TPU v7x, 32 devices: a whole 2x2x4 slice. The times are simulated.
32 devices in a mesh: tm: 16 (over z, y, x), batch: 2 (over core).
Axes of the slice: x: 2, y: 2, z: 4, core: 2. Of those that a mesh axis runs over, the one named last changes fastest.
Arguments:
- gate_in: bfloat16 [1024, 4096], P('tm', 'batch'), parts along dimension 1, may hold values from -4.5 to 8.75
- cand_in: bfloat16 [1024, 4096], P('tm', 'batch'), parts along dimension 1, may hold values from -6 to 6
- rates: float32 [4096], P('batch'), parts along dimension 0, may hold values from 9.765625e-05 to 0.5
- init_state: float32 [4096], P('batch'), parts along dimension 0, may hold values from -5 to 5
- recur_weight: bfloat16 [2048, 2048], replicated, may hold values from -0.5 to 0.5
Outputs:
- trajectory: float32 [1024, 4096], P('tm', 'batch'), parts along dimension 1
- step_norms: float32 [6], P('batch'), parts along dimension 0
There are 2 independent parts, one for each index of `batch`. A program takes and returns all parts, laid end to end along the dimension named above; an argument that names none is the same for every part. Nothing has to cross between parts.
All inputs are finite; a program needn't handle non-finite values.
Results may differ from a plain program's by a relative error of at most 0.0012.
Values sent between devices are 32-bit elements; how exact they have to be, the bound alone decides.
No kernel may reach another device: no remote copies, remote signals or barrier semaphores. Data moves between devices by JAX's collectives and lax.ppermute only.
A program may use at most 64 MiB of HBM per device.

v0:
```python
import jax
import jax.numpy as jnp
from jax import lax
from jax.sharding import PartitionSpec as P

ITERS = 3


def carried_in(x, axis, combine, identity):
    peers, place = (lax.axis_size(axis), lax.axis_index(axis))
    everything = jax.tree.map(lambda part: lax.all_gather(part, axis), x)
    start = jax.tree.map(
        lambda part, zero: jnp.broadcast_to(jnp.asarray(zero, part.dtype), part.shape), x, identity
    )

    def turn(k, before):
        reached = k < place
        new = combine(before, jax.tree.map(lambda part: part[k], everything))
        return jax.tree.map(lambda a, b: jnp.where(reached, a, b), new, before)

    return lax.fori_loop(0, peers, turn, start)


def link(earlier, later):
    return (later[0] * earlier[0], later[0] * earlier[1] + later[1])


def body(gate_in, cand_in, rates, init_state, recur_weight):
    rows, width = gate_in.shape
    devices = lax.axis_size("tm")
    first = lax.axis_index("tm") == 0
    gate = gate_in.astype(jnp.float32)
    keep = jnp.exp(-rates[None, :] * jax.nn.softplus(gate) - jnp.maximum(gate - 8.0, 0.0))
    cand_base = cand_in.astype(jnp.float32)
    unit_diag = jnp.diagonal(recur_weight).astype(jnp.float32)
    state = jnp.zeros((rows, width), jnp.float32)
    entry = jnp.where(first, init_state, jnp.zeros_like(init_state))
    ones = jnp.ones((width,), jnp.float32)
    zeros = jnp.zeros((width,), jnp.float32)
    totals = []
    for step in range(ITERS):
        before = entry
        prev = jnp.concatenate([before[None, :], state[: rows - 1]], axis=0)
        mixed = jnp.dot(prev.astype(jnp.bfloat16), recur_weight, preferred_element_type=jnp.float32)
        cand = jnp.tanh(cand_base + mixed)
        mapped = keep * prev + (1.0 - keep) * cand
        slope = keep + (1.0 - keep) * (1.0 - cand * cand) * unit_diag[None, :]
        offset = mapped - slope * prev
        cum_a, cum_b = lax.associative_scan(link, (slope, offset), axis=0)
        reach_a, reach_b = carried_in((cum_a[rows - 1], cum_b[rows - 1]), "tm", link, (ones, zeros))
        entry = reach_a * init_state + reach_b
        fresh = cum_b + cum_a * entry[None, :]
        delta = fresh - state
        local = jnp.sum(delta * delta)
        totals.append(lax.psum(local, "tm"))
        state = fresh
    summed = jnp.stack(totals)
    return (state, jnp.sqrt(summed / (rows * devices * width)))


def solution(mesh):
    placed = (P("tm", "batch"), P("tm", "batch"), P("batch"), P("batch"), P())
    return jax.shard_map(
        body, mesh=mesh, in_specs=placed, out_specs=(P("tm", "batch"), P("batch")), check_vma=False
    )
```

profile of v0, /device:TPU:0, one launch (start us, length us, event | category | flops | bytes accessed | tf_op | source)
XLA Modules:
  0.0 353.1 jit_solution(8567465255322649778)
XLA Ops:
  0.6 0.7 broadcast_select_fusion
  1.3 0.7 neg.8
  2.1 32.0 %gather_fusion = bf16[2048]{0:T(1024)(128)(2,1)S(1)} fusion(bf16[2048,2048]{1,0:T(8,128)(2,1)} %param.15, s32[2048]{0:T(1024)S(1)} %bitcast.60), kind=kCustom, calls=%fused_computation | custom fusion | bytes 24576 | tf_op jit(solution)/shard_map/jit(diagonal)/cond/branch_0_fun/gather | solution.py:35
  34.2 5.5 %multiply_add_fusion.5 = (f32[64,2048]{1,0:T(8,128)S(1)}, f32[64,2048]{1,0:T(8,128)S(1)}) fusion(f32[2048]{0:T(1024)S(1)} %convert_element_type.25, bf16[64,2048]{1,0:T(8,128)(2,1)} %param.11, f32[2048]{0:T(1024)S(1)} %neg.8, f32[1,2048]{1,0:T(1,128)S(1)} %bitcast.77, bf16[2048,2048]{1,0:T(8,128)(2,1)} %param.15, bf16[64,2048]{1,0:T(8,128)(2,1)} %param.12), kind=kOutput, calls=%fused_computation.48 | convolution fusion | flops 540016640 | bytes 9986048 | tf_op jit(solution)/shard_map/dot_general | solution.py:44
  39.8 0.1 slice.538
  39.9 0.1 slice.537
  40.1 0.2 slice.536
  40.3 0.2 slice.589
  40.6 0.1 slice.564
  43.6 42.4 %all-gather = f32[16,1,2048]{2,1,0:T(1,128)S(1)} all-gather(f32[1,1,2048]{2,1,0:T(1,128)S(1)} %add_bitcast_fusion.5), channel_id=1, replica_groups=mesh['tm'=16,'batch'=2] {'tm'}, dimensions={0}, use_global_device_ids=true | all-gather | bytes 139264 | tf_op jit(solution)/shard_map/all_gather | solution.py:11
  86.1 36.1 %all-gather.1 = f32[16,1,2048]{2,1,0:T(1,128)S(1)} all-gather(f32[1,1,2048]{2,1,0:T(1,128)S(1)} %add_bitcast_fusion.4), channel_id=1, replica_groups=mesh['tm'=16,'batch'=2] {'tm'}, dimensions={0}, use_global_device_ids=true | all-gather | bytes 139264 | tf_op jit(solution)/shard_map/all_gather | solution.py:11
  122.3 1.1 while.48
  123.6 5.5 %multiply_add_fusion.3 = (f32[64,2048]{1,0:T(8,128)S(1)}, f32[64,2048]{1,0:T(8,128)S(1)}) fusion(f32[2048]{0:T(1024)S(1)} %convert_element_type.25, bf16[64,2048]{1,0:T(8,128)(2,1)S(1)} %copy-done, f32[2048]{0:T(1024)S(1)} %neg.8, f32[63,2048]{1,0:T(8,128)S(1)} %bitcast.61, f32[1,2048]{1,0:T(1,128)S(1)} %bitcast.76, bf16[2048,2048]{1,0:T(8,128)(2,1)} %param.15, ...), kind=kOutput, calls=%fused_computation.46 | convolution fusion | flops 540672000 | bytes 10502144 | tf_op jit(solution)/shard_map/dot_general | solution.py:44
  129.3 0.1 slice.594
  129.4 0.2 slice.593
  129.6 0.2 slice.646
  132.9 38.2 %all-gather.2 = f32[16,1,2048]{2,1,0:T(1,128)S(1)} all-gather(f32[1,1,2048]{2,1,0:T(1,128)S(1)} %add_bitcast_fusion.3), channel_id=1, replica_groups=mesh['tm'=16,'batch'=2] {'tm'}, dimensions={0}, use_global_device_ids=true | all-gather | bytes 139264 | tf_op jit(solution)/shard_map/all_gather | solution.py:11
  171.1 0.7 copy.22
  171.9 36.4 %all-gather.3 = f32[16,1,2048]{2,1,0:T(1,128)S(1)} all-gather(f32[1,1,2048]{2,1,0:T(1,128)S(1)} %add_bitcast_fusion.2), channel_id=1, replica_groups=mesh['tm'=16,'batch'=2] {'tm'}, dimensions={0}, use_global_device_ids=true | all-gather | bytes 139264 | tf_op jit(solution)/shard_map/all_gather | solution.py:11
  208.3 14.4 %while.49 = (s32[]{:T(128)}, f32[2048]{0:T(1024)S(1)}, f32[2048]{0:T(1024)S(1)}, s32[]{:T(128)}, f32[16,2048]{1,0:T(8,128)}, /*index=5*/f32[16,2048]{1,0:T(8,128)S(1)}, s32[]{:T(128)}, s32[]{:T(128)}) while((s32[]{:T(128)}, f32[2048]{0:T(1024)S(1)}, f32[2048]{0:T(1024)S(1)}, s32[]{:T(128)}, f32[16,2048]{1,0:T(8,128)}, ...), condition=%wide.region_3.4_spmd.clone, body=%wide.region_2.3_spmd.clone.sunk | while | flops 14340 | bytes 82037 | solution.py:21
  208.4 0.9 constant_dynamic-slice_fusion.10
  209.3 0.9 constant_dynamic-slice_fusion.10
  210.2 0.9 constant_dynamic-slice_fusion.10
  211.1 0.9 constant_dynamic-slice_fusion.10
  212.0 0.9 constant_dynamic-slice_fusion.10
  212.9 0.9 constant_dynamic-slice_fusion.10
  213.8 0.9 constant_dynamic-slice_fusion.10
  214.7 0.9 constant_dynamic-slice_fusion.10
  215.6 0.9 constant_dynamic-slice_fusion.10
  216.5 0.9 constant_dynamic-slice_fusion.10
  217.4 0.9 constant_dynamic-slice_fusion.10
  218.3 0.9 constant_dynamic-slice_fusion.10
  219.2 0.9 constant_dynamic-slice_fusion.10
  220.1 0.9 constant_dynamic-slice_fusion.10
  221.0 0.9 constant_dynamic-slice_fusion.10
  221.9 0.9 constant_dynamic-slice_fusion.10
  222.8 1.2 multiply_add_fusion.2
  223.9 5.5 %multiply_subtract_fusion = (f32[64,2048]{1,0:T(8,128)S(1)}, f32[64,2048]{1,0:T(8,128)S(1)}) fusion(f32[63,2048]{1,0:T(8,128)S(1)} %bitcast.62, f32[1,2048]{1,0:T(1,128)S(1)} %bitcast.75, f32[2048]{0:T(1024)S(1)} %convert_element_type.25, bf16[64,2048]{1,0:T(8,128)(2,1)S(1)} %copy-done, f32[2048]{0:T(1024)S(1)} %neg.8, bf16[2048,2048]{1,0:T(8,128)(2,1)} %param.15, ...), kind=kOutput, calls=%fused_computation.42 | convolution fusion | flops 540672000 | bytes 10502144 | tf_op jit(solution)/shard_map/dot_general | solution.py:44
  229.4 0.2 slice.691
  229.9 0.1 slice.655
  230.3 0.2 slice.650
  233.2 38.3 %all-gather.5 = f32[16,1,2048]{2,1,0:T(1,128)S(1)} all-gather(f32[1,1,2048]{2,1,0:T(1,128)S(1)} %add_bitcast_fusion), channel_id=1, replica_groups=mesh['tm'=16,'batch'=2] {'tm'}, dimensions={0}, use_global_device_ids=true | all-gather | bytes 139264 | tf_op jit(solution)/shard_map/all_gather | solution.py:11
  271.7 36.1 %all-gather.4 = f32[16,1,2048]{2,1,0:T(1,128)S(1)} all-gather(f32[1,1,2048]{2,1,0:T(1,128)S(1)} %add_bitcast_fusion.1), channel_id=1, replica_groups=mesh['tm'=16,'batch'=2] {'tm'}, dimensions={0}, use_global_device_ids=true | all-gather | bytes 139264 | tf_op jit(solution)/shard_map/all_gather | solution.py:11
  307.8 1.1 while.50
  308.9 0.7 multiply_add_fusion.21
  309.7 1.7 multiply_reduce_fusion.2
  311.3 39.3 %all-reduce.73 = (f32[1]{0:T(128)}, f32[1]{0:T(128)}, f32[1]{0:T(128)}) all-reduce(f32[1]{0:T(128)} %bitcast.12, f32[1]{0:T(128)} %bitcast.11, f32[1]{0:T(128)} %bitcast.10), channel_id=1, replica_groups=mesh['tm'=16,'batch'=2] {'tm'}, use_global_device_ids=true, to_apply=%region_11.12 | all-reduce | flops 3 | bytes 24 | tf_op jit(solution)/shard_map/psum | solution.py:55
  350.6 2.5 fusion.41
  (358 shorter events, 9.7 us)
Async XLA Ops:
  42.0 81.5 %copy-start.3 = (f32[2048]{0:T(1024)S(1)}, f32[2048]{0:T(1024)}, u32[]{:S(2)}) copy-start(f32[2048]{0:T(1024)} %param.14) | copy-start | bytes 24580
  42.6 81.0 %copy-start = (bf16[64,2048]{1,0:T(8,128)(2,1)S(1)}, bf16[64,2048]{1,0:T(8,128)(2,1)}, u32[]{:S(2)}) copy-start(bf16[64,2048]{1,0:T(8,128)(2,1)} %param.11) | copy-start | bytes 786436
  42.6 81.0 %copy-start.1 = (bf16[64,2048]{1,0:T(8,128)(2,1)S(1)}, bf16[64,2048]{1,0:T(8,128)(2,1)}, u32[]{:S(2)}) copy-start(bf16[64,2048]{1,0:T(8,128)(2,1)} %param.12) | copy-start | bytes 786436
  171.9 50.8 %copy-start.2 = (f32[64,2048]{1,0:T(8,128)}, f32[64,2048]{1,0:T(8,128)S(1)}, u32[]{:S(2)}) copy-start(f32[64,2048]{1,0:T(8,128)S(1)} %pad.270) | copy-start | bytes 1572868
where the time goes:
time: 355 us; the launch traced here: 353 us
  blocking collectives  267 us (75%)
  local copies, waits for them, and re-layouts  55 us (15%)
  matrix products  16.5 us (5%)
  other arithmetic  10.5 us (3%)
    all_gather x6, blocking collectives, carried_in(): everything = jax.tree.map(lambda part: lax.all_gather(part, axis), x)  228 us
    psum x1, blocking collectives, body(): totals.append(lax.psum(local, 'tm'))  39.3 us
    gather x1, local copies, waits for them, and re-layouts, body(): unit_diag = jnp.diagonal(recur_weight).astype(jnp.float32)  32 us
    dot_general x3, matrix products, body(): jnp.dot(prev.astype(jnp.bfloat16), recur_weight, preferred_element_type=j...  16.5 us
    dynamic_slice x48, local copies, waits for them, and re-layouts, turn(): new = combine(before, jax.tree.map(lambda part: part[k], everything))  14.4 us

commit v1 on v0

v1 whole, which is shorter than its diff:
```python
import functools

import jax
import jax.numpy as jnp
from jax import lax
from jax.experimental import pallas as pl
from jax.experimental.pallas import tpu as pltpu
from jax.sharding import PartitionSpec as P

SUB = 8
LANE = 128
WIDE = 256
VMEM_LIMIT = 16 * 1024 * 1024
F32 = jnp.float32
BF16 = jnp.bfloat16


def softplus(x):
    return jnp.maximum(x, 0.0) + jnp.log1p(jnp.exp(-jnp.abs(x)))


def chunk_scan(mul, add):
    run_a, run_b = [mul[0]], [add[0]]
    for a, b in zip(mul[1:], add[1:]):
        run_a.append(a * run_a[-1])
        run_b.append(a * run_b[-1] + b)
    tot_a, tot_b = run_a[-1], run_b[-1]
    place = lax.broadcasted_iota(jnp.int32, tot_a.shape, 0)
    shift = 1
    while shift < SUB:
        far = place >= shift
        old_a = jnp.where(far, pltpu.roll(tot_a, shift, 0), 1.0)
        old_b = jnp.where(far, pltpu.roll(tot_b, shift, 0), 0.0)
        tot_b = tot_a * old_b + tot_b
        tot_a = tot_a * old_a
        shift *= 2
    far = place >= 1
    head_a = jnp.where(far, pltpu.roll(tot_a, 1, 0), 1.0)
    head_b = jnp.where(far, pltpu.roll(tot_b, 1, 0), 0.0)
    cum_a = [a * head_a for a in run_a]
    cum_b = [a * head_b + b for a, b in zip(run_a, run_b)]
    return cum_a, cum_b


def write_rows(ref, base, first_tile, row):
    for k in range(row.shape[1] // LANE):
        ref[pl.ds(base + first_tile + k, 1), :] = row[:, k * LANE : (k + 1) * LANE]


def read_row(ref, first_tile, tiles):
    return jnp.concatenate([ref[pl.ds(first_tile + k, 1), :] for k in range(tiles)], axis=1)


def spread(one_ref, out_ref):
    value = one_ref[...]
    for q in range(out_ref.shape[0]):
        out_ref[q] = value


def start_kernel(
    me_ref, gate_ref, cand_ref, rates_ref, init_ref, w_hbm,
    w_ref, keep_ref, base_ref, cum_a_ref, cum_b_ref, diag_ref, pay_ref,
    blocks, keep_nat, base_nat, mul_nat, add_nat, one, w_sem, d_sem,
):
    rows, width = gate_ref.shape
    steps = rows // SUB
    tiles = width // LANE
    parts = 8
    part = width // parts
    diag_copies = [
        pltpu.make_async_copy(
            w_hbm.at[pl.ds(k * LANE, LANE), pl.ds(k * LANE, LANE)], blocks.at[k], d_sem.at[k]
        )
        for k in range(tiles)
    ]
    w_copies = [
        pltpu.make_async_copy(
            w_hbm.at[pl.ds(k * part, part), :], w_ref.at[pl.ds(k * part, part), :], w_sem.at[k]
        )
        for k in range(parts)
    ]
    for copy in diag_copies:
        copy.start()
    for copy in w_copies:
        copy.start()

    per = WIDE // LANE

    def split(ref, j, value):
        for k in range(per):
            ref[j * per + k] = value[:, k * LANE : (k + 1) * LANE]

    def joined(ref, j, at):
        return jnp.concatenate([ref[j * per + k, at, :] for k in range(per)], axis=1)

    @pl.loop(0, width // WIDE)
    def _(j):
        cols = pl.ds(pl.multiple_of(j * WIDE, WIDE), WIDE)
        gate = gate_ref[:, cols].astype(F32)
        split(keep_nat, j, jnp.exp(-rates_ref[:, cols] * softplus(gate) - jnp.maximum(gate - 8.0, 0.0)))

    for copy in diag_copies:
        copy.wait()
    on_diag = lax.broadcasted_iota(jnp.int32, (LANE, LANE), 0) == lax.broadcasted_iota(jnp.int32, (LANE, LANE), 1)
    for k in range(tiles):
        block = blocks[k].astype(F32)
        diag_ref[:, k * LANE : (k + 1) * LANE] = jnp.sum(jnp.where(on_diag, block, 0.0), axis=0, keepdims=True)

    @pl.loop(0, width // WIDE)
    def _(j):
        cols = pl.ds(pl.multiple_of(j * WIDE, WIDE), WIDE)
        keep = joined(keep_nat, j, slice(None))
        base = cand_ref[:, cols].astype(F32)
        cand = jnp.tanh(base)
        left = 1.0 - keep
        split(mul_nat, j, keep + left * (1.0 - cand * cand) * diag_ref[:, cols])
        split(add_nat, j, left * cand)
        split(base_nat, j, base)

    @pl.when(me_ref[0] == 0)
    def _():
        total = jnp.zeros((SUB, width), F32)
        for k in range(parts):
            w_copies[k].wait()
            left = jnp.broadcast_to(init_ref[:, k * part : (k + 1) * part], (SUB, part)).astype(BF16)
            total = total + jnp.dot(left, w_ref[k * part : (k + 1) * part, :], preferred_element_type=F32)
        for j in range(tiles):
            here = slice(j * LANE, (j + 1) * LANE)
            prev = init_ref[:, here]
            keep = keep_nat[j, 0:1, :]
            cand = jnp.tanh(base_nat[j, 0:1, :] + total[0:1, here])
            mapped = keep * prev + (1.0 - keep) * cand
            slope = keep + (1.0 - keep) * (1.0 - cand * cand) * diag_ref[:, here]
            mul_nat[j, 0:1, :] = slope
            add_nat[j, 0:1, :] = mapped - slope * prev

    @pl.when(me_ref[0] != 0)
    def _():
        for copy in w_copies:
            copy.wait()

    @pl.loop(0, width // WIDE)
    def _(j):
        cols = pl.ds(pl.multiple_of(j * WIDE, WIDE), WIDE)
        turn = [pl.ds(r, SUB, stride=steps) for r in range(steps)]
        cum_a, cum_b = chunk_scan([joined(mul_nat, j, at) for at in turn], [joined(add_nat, j, at) for at in turn])
        for r in range(steps):
            here = pl.ds(r * SUB, SUB)
            cum_a_ref[here, cols] = cum_a[r]
            cum_b_ref[here, cols] = cum_b[r]
            keep_ref[here, cols] = joined(keep_nat, j, turn[r])
            base_ref[here, cols] = joined(base_nat, j, turn[r])
        write_rows(one, 0, j * per, cum_a[-1][SUB - 1 :, :])
        write_rows(one, tiles, j * per, cum_b[-1][SUB - 1 :, :])

    spread(one, pay_ref)


def step_kernel(
    last, me_ref, got_ref, init_ref, keep_ref, base_ref, cum_a_ref, cum_b_ref, diag_ref, w_ref, old_ref, tot_ref,
    *rest,
):
    if last:
        fresh_ref, out_a_ref, pay_ref, prev, low, entry, one, acc = rest
    else:
        state_ref, out_a_ref, out_b_ref, sum_ref, pay_ref, prev, low, entry, one, acc = rest
    rows, width = keep_ref.shape
    steps = rows // SUB
    tiles = width // LANE
    per = WIDE // LANE

    def pull(q, e):
        return got_ref[q, 0:tiles, :] * e + got_ref[q, tiles : 2 * tiles, :]

    entry[...] = lax.fori_loop(0, me_ref[0], pull, init_ref[...])
    acc[...] = jnp.zeros_like(acc)

    def turned_state(j, _):
        cols = pl.ds(pl.multiple_of(j * WIDE, WIDE), WIDE)
        e = read_row(entry, j * per, per)
        state = [
            cum_b_ref[pl.ds(r * SUB, SUB), cols] + cum_a_ref[pl.ds(r * SUB, SUB), cols] * e for r in range(steps)
        ]
        place = lax.broadcasted_iota(jnp.int32, state[0].shape, 0)
        before = [jnp.where(place == 0, jnp.broadcast_to(e, state[0].shape), pltpu.roll(state[-1], 1, 0))] + state[:-1]
        moved = 0.0
        for r in range(steps):
            prev[pl.ds(r * SUB, SUB), cols] = before[r]
            change = state[r] if old_ref is None else state[r] - old_ref[pl.ds(r * SUB, SUB), cols]
            moved = moved + change * change
            if not last:
                state_ref[pl.ds(r * SUB, SUB), cols] = state[r]
        for r in range(0, steps, 2):
            low[pl.ds(r * SUB, 2 * SUB), cols] = jnp.concatenate(before[r : r + 2], axis=0).astype(BF16)
        acc[...] += sum(moved[:, k * LANE : (k + 1) * LANE] for k in range(per))
        return 0

    lax.fori_loop(0, width // WIDE, turned_state, 0)
    if not last:
        sum_ref[...] = acc[...]
    else:
        one[pl.ds(4 * tiles, SUB), :] = jnp.zeros((SUB, LANE), F32)
        one[pl.ds(4 * tiles, 1), :] = jnp.sum(tot_ref[...], axis=0, keepdims=True)
        one[pl.ds(4 * tiles + 1, 1), :] = jnp.sum(acc[...], axis=0, keepdims=True)
        acc[...] = jnp.zeros_like(acc)

    def solve(j, _):
        cols = pl.ds(pl.multiple_of(j * WIDE, WIDE), WIDE)
        mixed = jnp.dot(low[...], w_ref[:, cols], preferred_element_type=F32)
        unit = diag_ref[:, cols]
        mul, add = [], []
        for r in range(steps):
            here = pl.ds(r * SUB, SUB)
            keep = keep_ref[here, cols]
            before = prev[here, cols]
            cand = jnp.tanh(base_ref[here, cols] + mixed[r * SUB : (r + 1) * SUB, :])
            left = 1.0 - keep
            mapped = keep * before + left * cand
            slope = keep + left * (1.0 - cand * cand) * unit
            mul.append(slope)
            add.append(mapped - slope * before)
        cum_a, cum_b = chunk_scan(mul, add)
        if last:
            e = read_row(entry, j * per, per)
            c0, c1, c2 = 0.0, 0.0, 0.0
            for r in range(steps):
                here = pl.ds(r * SUB, SUB)
                fresh = cum_b[r] + cum_a[r] * e
                if r + 1 < steps:
                    state = prev[pl.ds((r + 1) * SUB, SUB), cols]
                else:
                    state = cum_b_ref[here, cols] + cum_a_ref[here, cols] * e
                u = fresh - state
                fresh_ref[here, cols] = fresh
                out_a_ref[here, cols] = cum_a[r]
                c0 = c0 + u * u
                c1 = c1 + u * cum_a[r]
                c2 = c2 + cum_a[r] * cum_a[r]
            acc[...] += sum(c0[:, k * LANE : (k + 1) * LANE] for k in range(per))
            write_rows(one, 0, j * per, cum_a[-1][SUB - 1 :, :])
            write_rows(one, tiles, j * per, u[SUB - 1 :, :])
            write_rows(one, 2 * tiles, j * per, 2.0 * jnp.sum(c1, axis=0, keepdims=True))
            write_rows(one, 3 * tiles, j * per, jnp.sum(c2, axis=0, keepdims=True))
        else:
            for r in range(steps):
                here = pl.ds(r * SUB, SUB)
                out_a_ref[here, cols] = cum_a[r]
                out_b_ref[here, cols] = cum_b[r]
            write_rows(one, 0, j * per, cum_a[-1][SUB - 1 :, :])
            write_rows(one, tiles, j * per, cum_b[-1][SUB - 1 :, :])
        return 0

    lax.fori_loop(0, width // WIDE, solve, 0)
    if last:
        one[pl.ds(4 * tiles + 2, 1), :] = jnp.sum(acc[...], axis=0, keepdims=True)
    spread(one, pay_ref)


def first_step_kernel(me, got, init, keep, base, cum_a, cum_b, diag, w, *rest):
    step_kernel(False, me, got, init, keep, base, cum_a, cum_b, diag, w, None, None, *rest)


def final_kernel(me_ref, got_ref, fresh_ref, cum_a_ref, path_ref, norm_ref, entry, nat, quad_ref):
    rows, width = fresh_ref.shape
    steps = rows // SUB
    tiles = width // LANE
    peers = got_ref.shape[0]
    quad_ref[...] = jnp.zeros_like(quad_ref)
    entry[...] = jnp.zeros_like(entry)

    def pull(q, carry):
        d, quad, sums = carry

        @pl.when(q == me_ref[0])
        def _():
            entry[...] = d

        a, b = got_ref[q, 0:tiles, :], got_ref[q, tiles : 2 * tiles, :]
        c1, c2 = got_ref[q, 2 * tiles : 3 * tiles, :], got_ref[q, 3 * tiles : 4 * tiles, :]
        quad = quad + d * (c1 + c2 * d)
        sums = sums + got_ref[q, 4 * tiles : 4 * tiles + SUB, :]
        return a * d + b, quad, sums

    _, quad, sums = lax.fori_loop(0, peers, pull, (entry[...], quad_ref[0:tiles, :], quad_ref[tiles:, :]))
    count = peers * rows * width
    extra = jnp.sum(quad, axis=0, keepdims=True)
    totals = [sums[0:1, :], sums[1:2, :], sums[2:3, :] + extra]
    for k, row in enumerate(totals):
        total = jnp.sum(row, axis=1, keepdims=True)
        norm_ref[k] = jnp.max(jnp.sqrt(total / count))

    @pl.loop(0, tiles)
    def _(j):
        cols = pl.ds(pl.multiple_of(j * LANE, LANE), LANE)
        e = entry[pl.ds(j, 1), :]
        for r in range(steps):
            here = pl.ds(r * SUB, SUB)
            nat[j, pl.ds(r, SUB, stride=steps), :] = fresh_ref[here, cols] + cum_a_ref[here, cols] * e
        path_ref[:, cols] = nat[j]


def exchange(pay):
    return lax.all_to_all(pay, "tm", 0, 0)


def body(gate_in, cand_in, rates, init_state, recur_weight):
    rows, width = gate_in.shape
    peers = lax.axis_size("tm")
    tiles = width // LANE
    steps = rows // SUB
    assert rows % (2 * SUB) == 0 and width % WIDE == 0
    me = lax.axis_index("tm").astype(jnp.int32).reshape(1)
    init_row = init_state.reshape(1, width)
    init_tile = init_state.reshape(tiles, LANE)
    vmem = pl.BlockSpec(memory_space=pltpu.VMEM)
    smem = pl.BlockSpec(memory_space=pltpu.SMEM)
    hbm = pl.BlockSpec(memory_space=pl.ANY)
    grid_f32 = jax.ShapeDtypeStruct((rows, width), F32)
    pay2 = jax.ShapeDtypeStruct((peers, 2 * tiles, LANE), F32)
    pay4 = jax.ShapeDtypeStruct((peers, 4 * tiles + SUB, LANE), F32)

    w, keep, base, cum_a, cum_b, diag, pay = pl.pallas_call(
        start_kernel,
        out_shape=(
            pltpu.VMEM((width, width), BF16),
            grid_f32, grid_f32, grid_f32, grid_f32,
            jax.ShapeDtypeStruct((1, width), F32),
            pay2,
        ),
        in_specs=[smem, vmem, vmem, vmem, vmem, hbm],
        out_specs=(vmem,) * 7,
        scratch_shapes=[
            pltpu.VMEM((tiles, LANE, LANE), BF16),
            pltpu.VMEM((tiles, rows, LANE), F32),
            pltpu.VMEM((tiles, rows, LANE), F32),
            pltpu.VMEM((tiles, rows, LANE), F32),
            pltpu.VMEM((tiles, rows, LANE), F32),
            pltpu.VMEM((2 * tiles, LANE), F32),
            pltpu.SemaphoreType.DMA((8,)),
            pltpu.SemaphoreType.DMA((tiles,)),
        ],
        compiler_params=pltpu.CompilerParams(vmem_limit_bytes=VMEM_LIMIT),
        name="start",
    )(me, gate_in, cand_in, rates.reshape(1, width), init_row, recur_weight)
    got = exchange(pay)

    scratch = [
        pltpu.VMEM((rows, width), F32),
        pltpu.VMEM((rows, width), BF16),
        pltpu.VMEM((tiles, LANE), F32),
    ]
    state, cum_a, cum_b, moved, pay = pl.pallas_call(
        first_step_kernel,
        out_shape=(grid_f32, grid_f32, grid_f32, jax.ShapeDtypeStruct((SUB, LANE), F32), pay2),
        in_specs=[smem] + [vmem] * 8,
        out_specs=(vmem,) * 5,
        scratch_shapes=scratch + [pltpu.VMEM((2 * tiles, LANE), F32), pltpu.VMEM((SUB, LANE), F32)],
        compiler_params=pltpu.CompilerParams(vmem_limit_bytes=VMEM_LIMIT),
        name="middle",
    )(me, got, init_tile, keep, base, cum_a, cum_b, diag, w)
    got = exchange(pay)

    fresh, cum_a, pay = pl.pallas_call(
        functools.partial(step_kernel, True),
        out_shape=(grid_f32, grid_f32, pay4),
        in_specs=[smem] + [vmem] * 10,
        out_specs=(vmem,) * 3,
        scratch_shapes=scratch + [pltpu.VMEM((4 * tiles + SUB, LANE), F32), pltpu.VMEM((SUB, LANE), F32)],
        compiler_params=pltpu.CompilerParams(vmem_limit_bytes=VMEM_LIMIT),
        name="last",
    )(me, got, init_tile, keep, base, cum_a, cum_b, diag, w, state, moved)
    got = exchange(pay)

    path, norms = pl.pallas_call(
        final_kernel,
        out_shape=(grid_f32, jax.ShapeDtypeStruct((3,), F32)),
        in_specs=[smem] + [vmem] * 3,
        out_specs=(vmem, smem),
        scratch_shapes=[
            pltpu.VMEM((tiles, LANE), F32),
            pltpu.VMEM((tiles, rows, LANE), F32),
            pltpu.VMEM((tiles + SUB, LANE), F32),
        ],
        compiler_params=pltpu.CompilerParams(vmem_limit_bytes=VMEM_LIMIT),
        name="final",
    )(me, got, fresh, cum_a)
    return path, norms


def solution(mesh):
    placed = (P("tm", "batch"), P("tm", "batch"), P("batch"), P("batch"), P())
    return jax.shard_map(
        body, mesh=mesh, in_specs=placed, out_specs=(P("tm", "batch"), P("batch")), check_vma=False
    )
```

time: 355 us -> 68.9 us (0.19)
  blocking collectives: 267 us -> 48.9 us
  local copies, waits for them, and re-layouts: 55 us -> 6.67 us
  matrix products: 16.5 us -> 0 us
  Pallas kernels: 0 us -> 12.3 us
  other arithmetic: 10.5 us -> 0 us
    all_gather x6 -> x0, blocking collectives: 228 us -> none  [carried_in(): everything = jax.tree.map(lambda part: lax.all_gather(part, axis), x)]
    all_to_all x0 -> x3, blocking collectives: none -> 48.9 us  [exchange(): return lax.all_to_all(pay, 'tm', 0, 0)]
    psum x1 -> x0, blocking collectives: 39.3 us -> none  [body(): totals.append(lax.psum(local, 'tm'))]
    gather x1 -> x0, local copies, waits for them, and re-layouts: 32 us -> none  [body(): unit_diag = jnp.diagonal(recur_weight).astype(jnp.float32)]
    dot_general x3 -> x0, matrix products: 16.5 us -> none  [body(): jnp.dot(prev.astype(jnp.bfloat16), recur_weight, preferred_element_type=j...]
    dynamic_slice x48 -> x0, local copies, waits for them, and re-layouts: 14.4 us -> none  [turn(): new = combine(before, jax.tree.map(lambda part: part[k], everything))]
    pallas_call x0 -> x4, Pallas kernels: none -> 12.3 us  [the longest x1 4.23 us: body(): pl.pallas_call(start_kernel, out_shape=(pltpu.VMEM((width, width), BF16),...]
    unnamed x14 -> x10, local copies, waits for them, and re-layouts: 0.92 us -> 6.67 us
where the time goes in v1:
time: 68.9 us; the launch traced here: 68.5 us
  blocking collectives  48.9 us (71%)
  Pallas kernels  12.3 us (18%)
  local copies, waits for them, and re-layouts  6.67 us (10%)
    all_to_all x3, blocking collectives, exchange(): return lax.all_to_all(pay, 'tm', 0, 0)  48.9 us
    unnamed x10, local copies, waits for them, and re-layouts  6.67 us
    pallas_call x1, Pallas kernels, body(): pl.pallas_call(start_kernel, out_shape=(pltpu.VMEM((width, width), BF16),...  4.23 us
    pallas_call x1, Pallas kernels, body(): pl.pallas_call(functools.partial(step_kernel, True), out_shape=(grid_f32,...  3.4 us
    pallas_call x1, Pallas kernels, body(): pl.pallas_call(first_step_kernel, out_shape=(grid_f32, grid_f32, grid_f32...  3.17 us
    pallas_call x1, Pallas kernels, body(): pl.pallas_call(final_kernel, out_shape=(grid_f32, jax.ShapeDtypeStruct((3...  1.49 us

profile of v1, /device:TPU:0, one launch (start us, length us, event | category | flops | bytes accessed | tf_op | source)
XLA Modules:
  0.0 68.5 jit_solution(16764426248926625702)
XLA Ops:
  0.6 0.0 copy-start
  0.6 3.4 %copy-done = bf16[2048,2048]{1,0:T(8,128)(2,1)S(1)} copy-done((bf16[2048,2048]{1,0:T(8,128)(2,1)S(1)}, bf16[2048,2048]{1,0:T(8,128)(2,1)}, u32[]{:S(2)}) %copy-start) | copy-done | bytes 8388632
  4.0 0.0 copy-start.1
  4.0 0.9 %copy-done.1 = bf16[64,2048]{1,0:T(8,128)(2,1)S(1)} copy-done((bf16[64,2048]{1,0:T(8,128)(2,1)S(1)}, bf16[64,2048]{1,0:T(8,128)(2,1)}, u32[]{:S(2)}) %copy-start.1) | copy-done | bytes 262168
  5.0 0.0 copy-start.2
  5.0 0.9 %copy-done.2 = bf16[64,2048]{1,0:T(8,128)(2,1)S(1)} copy-done((bf16[64,2048]{1,0:T(8,128)(2,1)S(1)}, bf16[64,2048]{1,0:T(8,128)(2,1)}, u32[]{:S(2)}) %copy-start.2) | copy-done | bytes 262168
  5.9 0.0 copy-start.3
  5.9 0.7 %copy-done.3 = f32[2048]{0:T(1024)S(1)} copy-done((f32[2048]{0:T(1024)S(1)}, f32[2048]{0:T(1024)}, u32[]{:S(2)}) %copy-start.3) | copy-done | bytes 8216
  6.6 0.0 copy-start.4
  6.6 0.7 %copy-done.4 = f32[2048]{0:T(1024)S(1)} copy-done((f32[2048]{0:T(1024)S(1)}, f32[2048]{0:T(1024)}, u32[]{:S(2)}) %copy-start.4) | copy-done | bytes 8216
  7.3 4.2 %start.1 = (bf16[2048,2048]{1,0:T(8,128)(2,1)S(1)}, f32[64,2048]{1,0:T(8,128)S(1)}, f32[64,2048]{1,0:T(8,128)S(1)}, f32[64,2048]{1,0:T(8,128)S(1)}, f32[64,2048]...) custom-call(s32[1]{0:T(128)} %bitcast.me_ref.me, bf16[64,2048]{1,0:T(8,128)(2,1)S(1)} %copy-done.1, ...), custom_call_target="tpu_custom_call" | custom-call | tf_op jit(solution)/shard_map/start/pallas_call | solution.py:322
  11.5 16.0 %all_to_all.15.got = f32[16,32,128]{2,1,0:T(8,128)S(1)} all-to-all(f32[16,32,128]{2,1,0:T(8,128)S(1)} %get-tuple-element.17), channel_id=1, replica_groups=mesh['tm'=16,'batch'=2] {'tm'}, dimensions={0} | all-to-all | bytes 524288 | tf_op jit(solution)/shard_map/all_to_all | solution.py:303
  27.6 3.2 %middle.1 = (f32[64,2048]{1,0:T(8,128)S(1)}, f32[64,2048]{1,0:T(8,128)S(1)}, f32[64,2048]{1,0:T(8,128)S(1)}, f32[8,128]{1,0:T(8,128)S(1)}, f32[16,32,128]{2,1,0:T(8,128)S(1)}) custom-call(s32[1]{0:T(128)} %bitcast.me_ref.me, f32[16,32,128]{2,1,0:T(8,128)S(1)} %all_to_all.15.got, f32[16,128]{1,0:T(8,128)S(1)} %bitcast.5, ...), custom_call_target="tpu_custom_call" | custom-call | tf_op jit(solution)/shard_map/middle/pallas_call | solution.py:352
  30.8 12.7 %all_to_all.16.got_ref = f32[16,32,128]{2,1,0:T(8,128)S(1)} all-to-all(f32[16,32,128]{2,1,0:T(8,128)S(1)} %get-tuple-element.24), channel_id=1, replica_groups=mesh['tm'=16,'batch'=2] {'tm'}, dimensions={0} | all-to-all | bytes 524288 | tf_op jit(solution)/shard_map/all_to_all | solution.py:303
  43.4 3.4 %last.1 = (f32[64,2048]{1,0:T(8,128)S(1)}, f32[64,2048]{1,0:T(8,128)S(1)}, f32[16,72,128]{2,1,0:T(8,128)S(1)}) custom-call(s32[1]{0:T(128)} %bitcast.me_ref.me, f32[16,32,128]{2,1,0:T(8,128)S(1)} %all_to_all.16.got_ref, f32[16,128]{1,0:T(8,128)S(1)} %bitcast.6, f32[64,2048]{1,0:T(8,128)S(1)} %get-tuple-element.18.keep.keep_ref, ...), custom_call_target="tpu_custom_call" | custom-call | tf_op jit(solution)/shard_map/last/pallas_call | solution.py:363
  46.8 20.2 %all_to_all.17.got_ref = f32[16,72,128]{2,1,0:T(8,128)S(1)} all-to-all(f32[16,72,128]{2,1,0:T(8,128)S(1)} %get-tuple-element.29), channel_id=1, replica_groups=mesh['tm'=16,'batch'=2] {'tm'}, dimensions={0} | all-to-all | bytes 1179648 | tf_op jit(solution)/shard_map/all_to_all | solution.py:303
  67.0 1.5 %final.1 = (f32[64,2048]{1,0:T(8,128)}, f32[3]{0:T(128)}) custom-call(s32[1]{0:T(128)} %bitcast.me_ref.me, f32[16,72,128]{2,1,0:T(8,128)S(1)} %all_to_all.17.got_ref, f32[64,2048]{1,0:T(8,128)S(1)} %get-tuple-element.30.fresh_ref, f32[64,2048]{1,0:T(8,128)S(1)} %get-tuple-element.31.cum_a_ref), custom_call_target="tpu_custom_call" | custom-call | tf_op jit(solution)/shard_map/final/pallas_call | solution.py:374
Async XLA Ops:
  0.6 3.4 %copy-start = (bf16[2048,2048]{1,0:T(8,128)(2,1)S(1)}, bf16[2048,2048]{1,0:T(8,128)(2,1)}, u32[]{:S(2)}) copy-start(bf16[2048,2048]{1,0:T(8,128)(2,1)} %w_hbm.1) | copy-start | bytes 25165828
  4.0 0.9 %copy-start.1 = (bf16[64,2048]{1,0:T(8,128)(2,1)S(1)}, bf16[64,2048]{1,0:T(8,128)(2,1)}, u32[]{:S(2)}) copy-start(bf16[64,2048]{1,0:T(8,128)(2,1)} %gate_ref.1) | copy-start | bytes 786436
  5.0 0.9 %copy-start.2 = (bf16[64,2048]{1,0:T(8,128)(2,1)S(1)}, bf16[64,2048]{1,0:T(8,128)(2,1)}, u32[]{:S(2)}) copy-start(bf16[64,2048]{1,0:T(8,128)(2,1)} %cand_ref.1) | copy-start | bytes 786436
  5.9 0.7 %copy-start.3 = (f32[2048]{0:T(1024)S(1)}, f32[2048]{0:T(1024)}, u32[]{:S(2)}) copy-start(f32[2048]{0:T(1024)} %param.8) | copy-start | bytes 24580
  6.6 0.7 %copy-start.4 = (f32[2048]{0:T(1024)S(1)}, f32[2048]{0:T(1024)}, u32[]{:S(2)}) copy-start(f32[2048]{0:T(1024)} %param.7) | copy-start | bytes 24580

commit v2 on v1

v2 whole, which is shorter than its diff:
```python
import functools

import jax
import jax.numpy as jnp
from jax import lax
from jax.experimental import pallas as pl
from jax.experimental.pallas import tpu as pltpu
from jax.sharding import PartitionSpec as P

SUB = 8
LANE = 128
WIDE = 256
PARTS = 4
VMEM_LIMIT = 16 * 1024 * 1024
F32 = jnp.float32
BF16 = jnp.bfloat16


def softplus(x):
    return jnp.maximum(x, 0.0) + jnp.log1p(jnp.exp(-jnp.abs(x)))


def chunk_scan(mul, add):
    run_a, run_b = [mul[0]], [add[0]]
    for a, b in zip(mul[1:], add[1:]):
        run_a.append(a * run_a[-1])
        run_b.append(a * run_b[-1] + b)
    tot_a, tot_b = run_a[-1], run_b[-1]
    place = lax.broadcasted_iota(jnp.int32, tot_a.shape, 0)
    shift = 1
    while shift < SUB:
        far = place >= shift
        old_a = jnp.where(far, pltpu.roll(tot_a, shift, 0), 1.0)
        old_b = jnp.where(far, pltpu.roll(tot_b, shift, 0), 0.0)
        tot_b = tot_a * old_b + tot_b
        tot_a = tot_a * old_a
        shift *= 2
    far = place >= 1
    head_a = jnp.where(far, pltpu.roll(tot_a, 1, 0), 1.0)
    head_b = jnp.where(far, pltpu.roll(tot_b, 1, 0), 0.0)
    cum_a = [a * head_a for a in run_a]
    cum_b = [a * head_b + b for a, b in zip(run_a, run_b)]
    return cum_a, cum_b


def write_rows(ref, base, first_tile, row):
    for k in range(row.shape[1] // LANE):
        ref[pl.ds(base + first_tile + k, 1), :] = row[:, k * LANE : (k + 1) * LANE]


def read_row(ref, first_tile, tiles):
    return jnp.concatenate([ref[pl.ds(first_tile + k, 1), :] for k in range(tiles)], axis=1)


def spread(one_ref, out_ref):
    value = one_ref[...]
    for q in range(out_ref.shape[0]):
        out_ref[q] = value


def start_kernel(
    me_ref, gate_hbm, cand_hbm, rates_hbm, init_hbm, w_hbm,
    keep_ref, base_ref, cum_a_ref, cum_b_ref, diag_ref, pay_ref,
    gate_ref, cand_ref, rates_ref, init_ref, w_ref, blocks, gate_nat, base_nat, mixed, one,
    in_sem, w_sem, d_sem,
):
    rows, width = gate_ref.shape
    steps = rows // SUB
    tiles = width // LANE
    per = WIDE // LANE
    part = width // PARTS
    me = me_ref[0]

    def columns(hbm, ref, k, sem):
        cols = pl.ds(k * part, part)
        return pltpu.make_async_copy(hbm.at[:, cols], ref.at[:, cols], sem)

    rates_copy = pltpu.make_async_copy(rates_hbm, rates_ref, in_sem.at[2 * PARTS])
    init_copy = pltpu.make_async_copy(init_hbm, init_ref, in_sem.at[2 * PARTS + 1])
    gate_copies = [columns(gate_hbm, gate_ref, k, in_sem.at[k]) for k in range(PARTS)]
    cand_copies = [columns(cand_hbm, cand_ref, k, in_sem.at[PARTS + k]) for k in range(PARTS)]
    diag_copies = [
        pltpu.make_async_copy(
            w_hbm.at[pl.ds(k * LANE, LANE), pl.ds(k * LANE, LANE)], blocks.at[k], d_sem.at[k]
        )
        for k in range(tiles)
    ]
    w_copies = [
        pltpu.make_async_copy(
            w_hbm.at[pl.ds(k * part, part), :], w_ref.at[pl.ds(k * part, part), :], w_sem.at[k]
        )
        for k in range(PARTS)
    ]
    rates_copy.start()
    for k in range(PARTS):
        gate_copies[k].start()
        cand_copies[k].start()
    init_copy.start()
    for copy in diag_copies:
        copy.start()

    @pl.when(me == 0)
    def _():
        for copy in w_copies:
            copy.start()

    mixed[...] = jnp.zeros_like(mixed)
    rates_copy.wait()
    turn = [pl.ds(r, SUB, stride=steps) for r in range(steps)]
    for k in range(PARTS):
        gate_copies[k].wait()
        cand_copies[k].wait()

        @pl.loop(k * (part // LANE), (k + 1) * (part // LANE))
        def _(j):
            cols = pl.ds(pl.multiple_of(j * LANE, LANE), LANE)
            gate_nat[j] = gate_ref[:, cols].astype(F32)
            base_nat[j] = cand_ref[:, cols].astype(F32)
            rate = rates_ref[:, cols]
            for r in range(steps):
                here = pl.ds(r * SUB, SUB)
                gate = gate_nat[j, turn[r], :]
                keep_ref[here, cols] = jnp.exp(-rate * softplus(gate) - jnp.maximum(gate - 8.0, 0.0))
                base_ref[here, cols] = base_nat[j, turn[r], :]

    for copy in diag_copies:
        copy.wait()
    on_diag = lax.broadcasted_iota(jnp.int32, (LANE, LANE), 0) == lax.broadcasted_iota(jnp.int32, (LANE, LANE), 1)
    for k in range(tiles):
        block = blocks[k].astype(F32)
        diag_ref[:, k * LANE : (k + 1) * LANE] = jnp.sum(jnp.where(on_diag, block, 0.0), axis=0, keepdims=True)
    init_copy.wait()

    @pl.when(me == 0)
    def _():
        total = jnp.zeros((SUB, width), F32)
        for k in range(PARTS):
            w_copies[k].wait()
            left = jnp.broadcast_to(init_ref[:, k * part : (k + 1) * part], (SUB, part)).astype(BF16)
            total = total + jnp.dot(left, w_ref[k * part : (k + 1) * part, :], preferred_element_type=F32)
        mixed[...] = total[0:1, :]

    @pl.when(me != 0)
    def _():
        init_ref[...] = jnp.zeros_like(init_ref)

    @pl.loop(0, width // WIDE)
    def _(j):
        cols = pl.ds(pl.multiple_of(j * WIDE, WIDE), WIDE)
        top = lax.broadcasted_iota(jnp.int32, (SUB, WIDE), 0) == 0
        unit = diag_ref[:, cols]
        mul, add = [], []
        for r in range(steps):
            here = pl.ds(r * SUB, SUB)
            keep = keep_ref[here, cols]
            left = 1.0 - keep
            base = base_ref[here, cols]
            cand = jnp.tanh(base + jnp.where(top, mixed[:, cols], 0.0) if r == 0 else base)
            slope = keep + left * (1.0 - cand * cand) * unit
            offset = left * cand
            if r == 0:
                prev = jnp.where(top, init_ref[:, cols], 0.0)
                offset = (keep * prev + offset) - slope * prev
            mul.append(slope)
            add.append(offset)
        cum_a, cum_b = chunk_scan(mul, add)
        for r in range(steps):
            here = pl.ds(r * SUB, SUB)
            cum_a_ref[here, cols] = cum_a[r]
            cum_b_ref[here, cols] = cum_b[r]
        write_rows(one, 0, j * per, cum_a[-1][SUB - 1 :, :])
        write_rows(one, tiles, j * per, cum_b[-1][SUB - 1 :, :])

    spread(one, pay_ref)


def step_kernel(
    last, me_ref, got_ref, init_ref, keep_ref, base_ref, cum_a_ref, cum_b_ref, diag_ref, w_ref, old_ref, tot_ref,
    *rest,
):
    if last:
        fresh_ref, out_a_ref, pay_ref, sums_ref, prev, low, entry, one, acc, more = rest
    else:
        state_ref, out_a_ref, out_b_ref, sum_ref, pay_ref, prev, low, entry, one, acc = rest
    rows, width = keep_ref.shape
    steps = rows // SUB
    tiles = width // LANE
    per = WIDE // LANE

    def pull(q, e):
        return got_ref[q, 0:tiles, :] * e + got_ref[q, tiles : 2 * tiles, :]

    entry[...] = lax.fori_loop(0, me_ref[0], pull, init_ref[...])
    acc[...] = jnp.zeros_like(acc)

    def turned_state(j, _):
        cols = pl.ds(pl.multiple_of(j * WIDE, WIDE), WIDE)
        e = read_row(entry, j * per, per)
        state = [
            cum_b_ref[pl.ds(r * SUB, SUB), cols] + cum_a_ref[pl.ds(r * SUB, SUB), cols] * e for r in range(steps)
        ]
        place = lax.broadcasted_iota(jnp.int32, state[0].shape, 0)
        before = [jnp.where(place == 0, jnp.broadcast_to(e, state[0].shape), pltpu.roll(state[-1], 1, 0))] + state[:-1]
        moved = 0.0
        for r in range(steps):
            prev[pl.ds(r * SUB, SUB), cols] = before[r]
            change = state[r] if old_ref is None else state[r] - old_ref[pl.ds(r * SUB, SUB), cols]
            moved = moved + change * change
            if not last:
                state_ref[pl.ds(r * SUB, SUB), cols] = state[r]
        for r in range(0, steps, 2):
            low[pl.ds(r * SUB, 2 * SUB), cols] = jnp.concatenate(before[r : r + 2], axis=0).astype(BF16)
        acc[...] += sum(moved[:, k * LANE : (k + 1) * LANE] for k in range(per))
        return 0

    lax.fori_loop(0, width // WIDE, turned_state, 0)
    if not last:
        sum_ref[...] = acc[...]
    else:
        more[pl.ds(2 * tiles, SUB), :] = jnp.zeros((SUB, LANE), F32)
        more[pl.ds(2 * tiles, 1), :] = jnp.sum(tot_ref[...], axis=0, keepdims=True)
        more[pl.ds(2 * tiles + 1, 1), :] = jnp.sum(acc[...], axis=0, keepdims=True)
        acc[...] = jnp.zeros_like(acc)

    def solve(j, _):
        cols = pl.ds(pl.multiple_of(j * WIDE, WIDE), WIDE)
        mixed = jnp.dot(low[...], w_ref[:, cols], preferred_element_type=F32)
        unit = diag_ref[:, cols]
        mul, add = [], []
        for r in range(steps):
            here = pl.ds(r * SUB, SUB)
            keep = keep_ref[here, cols]
            before = prev[here, cols]
            cand = jnp.tanh(base_ref[here, cols] + mixed[r * SUB : (r + 1) * SUB, :])
            left = 1.0 - keep
            mapped = keep * before + left * cand
            slope = keep + left * (1.0 - cand * cand) * unit
            mul.append(slope)
            add.append(mapped - slope * before)
        cum_a, cum_b = chunk_scan(mul, add)
        if last:
            e = read_row(entry, j * per, per)
            c0, c1, c2 = 0.0, 0.0, 0.0
            for r in range(steps):
                here = pl.ds(r * SUB, SUB)
                fresh = cum_b[r] + cum_a[r] * e
                if r + 1 < steps:
                    state = prev[pl.ds((r + 1) * SUB, SUB), cols]
                else:
                    state = cum_b_ref[here, cols] + cum_a_ref[here, cols] * e
                u = fresh - state
                fresh_ref[here, cols] = fresh
                out_a_ref[here, cols] = cum_a[r]
                c0 = c0 + u * u
                c1 = c1 + u * cum_a[r]
                c2 = c2 + cum_a[r] * cum_a[r]
            acc[...] += sum(c0[:, k * LANE : (k + 1) * LANE] for k in range(per))
            write_rows(one, 0, j * per, cum_a[-1][SUB - 1 :, :])
            write_rows(one, tiles, j * per, u[SUB - 1 :, :])
            write_rows(more, 0, j * per, 2.0 * jnp.sum(c1, axis=0, keepdims=True))
            write_rows(more, tiles, j * per, jnp.sum(c2, axis=0, keepdims=True))
        else:
            for r in range(steps):
                here = pl.ds(r * SUB, SUB)
                out_a_ref[here, cols] = cum_a[r]
                out_b_ref[here, cols] = cum_b[r]
            write_rows(one, 0, j * per, cum_a[-1][SUB - 1 :, :])
            write_rows(one, tiles, j * per, cum_b[-1][SUB - 1 :, :])
        return 0

    lax.fori_loop(0, width // WIDE, solve, 0)
    if last:
        more[pl.ds(2 * tiles + 2, 1), :] = jnp.sum(acc[...], axis=0, keepdims=True)
        spread(more, sums_ref)
    spread(one, pay_ref)


def first_step_kernel(me, got, init, keep, base, cum_a, cum_b, diag, w, *rest):
    step_kernel(False, me, got, init, keep, base, cum_a, cum_b, diag, w, None, None, *rest)


def path_kernel(me_ref, got_ref, fresh_ref, cum_a_ref, path_ref, moves_ref, nat):
    rows, width = fresh_ref.shape
    steps = rows // SUB
    tiles = width // LANE
    peers = got_ref.shape[0]
    moves_ref[0] = jnp.zeros((tiles, LANE), F32)

    def pull(q, d):
        d = got_ref[q, 0:tiles, :] * d + got_ref[q, tiles : 2 * tiles, :]
        moves_ref[q + 1] = d
        return d

    lax.fori_loop(0, peers - 1, pull, moves_ref[0])

    @pl.loop(0, tiles)
    def _(j):
        cols = pl.ds(pl.multiple_of(j * LANE, LANE), LANE)
        e = moves_ref[me_ref[0], pl.ds(j, 1), :]
        for r in range(steps):
            here = pl.ds(r * SUB, SUB)
            nat[j, pl.ds(r, SUB, stride=steps), :] = fresh_ref[here, cols] + cum_a_ref[here, cols] * e
        path_ref[:, cols] = nat[j]


def norm_kernel(count, moves_ref, sums_ref, norm_ref, quad_ref):
    peers, tiles, _ = moves_ref.shape
    quad_ref[...] = jnp.zeros_like(quad_ref)

    def gather(q, carry):
        quad, sums = carry
        d = moves_ref[q]
        quad = quad + d * (sums_ref[q, 0:tiles, :] + sums_ref[q, tiles : 2 * tiles, :] * d)
        return quad, sums + sums_ref[q, 2 * tiles : 2 * tiles + SUB, :]

    quad, sums = lax.fori_loop(0, peers, gather, (quad_ref[0:tiles, :], quad_ref[tiles:, :]))
    extra = jnp.sum(quad, axis=0, keepdims=True)
    totals = [sums[0:1, :], sums[1:2, :], sums[2:3, :] + extra]
    for k, row in enumerate(totals):
        total = jnp.sum(row, axis=1, keepdims=True)
        norm_ref[k] = jnp.max(jnp.sqrt(total / count))


def exchange(pay):
    return lax.all_to_all(pay, "tm", 0, 0)


def body(gate_in, cand_in, rates, init_state, recur_weight):
    rows, width = gate_in.shape
    peers = lax.axis_size("tm")
    tiles = width // LANE
    steps = rows // SUB
    assert rows % (2 * SUB) == 0 and width % WIDE == 0
    me = lax.axis_index("tm").astype(jnp.int32).reshape(1)
    init_row = init_state.reshape(1, width)
    init_tile = init_state.reshape(tiles, LANE)
    vmem = pl.BlockSpec(memory_space=pltpu.VMEM)
    smem = pl.BlockSpec(memory_space=pltpu.SMEM)
    hbm = pl.BlockSpec(memory_space=pltpu.HBM)
    grid_f32 = jax.ShapeDtypeStruct((rows, width), F32)
    pay2 = jax.ShapeDtypeStruct((peers, 2 * tiles, LANE), F32)
    pay3 = jax.ShapeDtypeStruct((peers, 2 * tiles + SUB, LANE), F32)

    keep, base, cum_a, cum_b, diag, pay = pl.pallas_call(
        start_kernel,
        out_shape=(grid_f32, grid_f32, grid_f32, grid_f32, jax.ShapeDtypeStruct((1, width), F32), pay2),
        in_specs=[smem] + [hbm] * 5,
        out_specs=(vmem,) * 6,
        scratch_shapes=[
            pltpu.VMEM((rows, width), BF16),
            pltpu.VMEM((rows, width), BF16),
            pltpu.VMEM((1, width), F32),
            pltpu.VMEM((1, width), F32),
            pltpu.VMEM((width, width), BF16),
            pltpu.VMEM((tiles, LANE, LANE), BF16),
            pltpu.VMEM((tiles, rows, LANE), F32),
            pltpu.VMEM((tiles, rows, LANE), F32),
            pltpu.VMEM((1, width), F32),
            pltpu.VMEM((2 * tiles, LANE), F32),
            pltpu.SemaphoreType.DMA((2 * PARTS + 2,)),
            pltpu.SemaphoreType.DMA((PARTS,)),
            pltpu.SemaphoreType.DMA((tiles,)),
        ],
        compiler_params=pltpu.CompilerParams(vmem_limit_bytes=VMEM_LIMIT),
        name="start",
    )(me, *(pltpu.with_memory_space_constraint(x, pltpu.HBM) for x in (gate_in, cand_in, rates.reshape(1, width), init_row, recur_weight)))
    got = exchange(pay)

    scratch = [
        pltpu.VMEM((rows, width), F32),
        pltpu.VMEM((rows, width), BF16),
        pltpu.VMEM((tiles, LANE), F32),
    ]
    state, cum_a, cum_b, moved, pay = pl.pallas_call(
        first_step_kernel,
        out_shape=(grid_f32, grid_f32, grid_f32, jax.ShapeDtypeStruct((SUB, LANE), F32), pay2),
        in_specs=[smem] + [vmem] * 8,
        out_specs=(vmem,) * 5,
        scratch_shapes=scratch + [pltpu.VMEM((2 * tiles, LANE), F32), pltpu.VMEM((SUB, LANE), F32)],
        compiler_params=pltpu.CompilerParams(vmem_limit_bytes=VMEM_LIMIT),
        name="middle",
    )(me, got, init_tile, keep, base, cum_a, cum_b, diag, recur_weight)
    got = exchange(pay)

    fresh, cum_a, pay, sums = pl.pallas_call(
        functools.partial(step_kernel, True),
        out_shape=(grid_f32, grid_f32, pay2, pay3),
        in_specs=[smem] + [vmem] * 10,
        out_specs=(vmem,) * 4,
        scratch_shapes=scratch
        + [
            pltpu.VMEM((2 * tiles, LANE), F32),
            pltpu.VMEM((SUB, LANE), F32),
            pltpu.VMEM((2 * tiles + SUB, LANE), F32),
        ],
        compiler_params=pltpu.CompilerParams(vmem_limit_bytes=VMEM_LIMIT),
        name="last",
    )(me, got, init_tile, keep, base, cum_a, cum_b, diag, recur_weight, state, moved)
    got = exchange(pay)
    sums = exchange(sums)

    path, moves = pl.pallas_call(
        path_kernel,
        out_shape=(grid_f32, jax.ShapeDtypeStruct((peers, tiles, LANE), F32)),
        in_specs=[smem] + [vmem] * 3,
        out_specs=(vmem,) * 2,
        scratch_shapes=[pltpu.VMEM((tiles, rows, LANE), F32)],
        compiler_params=pltpu.CompilerParams(vmem_limit_bytes=VMEM_LIMIT),
        cost_estimate=pl.CostEstimate(flops=10**10, bytes_accessed=2**21, transcendentals=0),
        name="path",
    )(me, got, fresh, cum_a)
    norms = pl.pallas_call(
        functools.partial(norm_kernel, peers * rows * width),
        out_shape=jax.ShapeDtypeStruct((3,), F32),
        in_specs=[vmem] * 2,
        out_specs=smem,
        scratch_shapes=[pltpu.VMEM((tiles + SUB, LANE), F32)],
        compiler_params=pltpu.CompilerParams(vmem_limit_bytes=VMEM_LIMIT),
        name="norm",
    )(moves, sums)
    return path, norms


def solution(mesh):
    placed = (P("tm", "batch"), P("tm", "batch"), P("batch"), P("batch"), P())
    return jax.shard_map(
        body, mesh=mesh, in_specs=placed, out_specs=(P("tm", "batch"), P("batch")), check_vma=False
    )
```

time: 68.9 us -> 69.5 us (level)
  waiting for transfers between devices: 0 us -> 9.37 us
  blocking collectives: 48.9 us -> 40.7 us
  local copies, waits for them, and re-layouts: 6.67 us -> 0.01 us
  starting transfers between devices: 0 us -> 3.55 us
  Pallas kernels: 12.3 us -> 14.9 us
    all_to_all x0 -> x1, waiting for transfers between devices: none -> 9.37 us  [exchange(): return lax.all_to_all(pay, 'tm', 0, 0)]
    all_to_all x3, blocking collectives: 48.9 us -> 40.7 us  [exchange(): return lax.all_to_all(pay, 'tm', 0, 0)]
    unnamed x10 -> x4, local copies, waits for them, and re-layouts: 6.67 us -> 0.01 us
    all_to_all x0 -> x1, starting transfers between devices: none -> 3.55 us  [exchange(): return lax.all_to_all(pay, 'tm', 0, 0)]
    pallas_call x2 -> x3, Pallas kernels: 5.71 us -> 7.6 us  [the longest x1 5.62 us: body(): pl.pallas_call(start_kernel, out_shape=(grid_f32, grid_f32, grid_f32, gri...]
    pallas_call x1, Pallas kernels: 3.4 us -> 4.13 us  [body(): pl.pallas_call(functools.partial(step_kernel, True), out_shape=(grid_f32,...]
  transfers between devices with their start and end apart: 0 -> 1, of which waited for: 0 -> 1; matrix products, arithmetic and copies ran while one was open for 0% -> 0% of each run, Pallas kernels for 0% -> 2%
where the time goes in v2:
time: 69.5 us; the launch traced here: 69.2 us
  blocking collectives  40.7 us (59%)
  Pallas kernels  14.9 us (21%)
  waiting for transfers between devices  9.37 us (13%)
  starting transfers between devices  3.55 us (5%)
    all_to_all x3, blocking collectives, exchange(): return lax.all_to_all(pay, 'tm', 0, 0)  40.7 us
    all_to_all x1, waiting for transfers between devices, exchange(): return lax.all_to_all(pay, 'tm', 0, 0)  9.37 us
    pallas_call x1, Pallas kernels, body(): pl.pallas_call(start_kernel, out_shape=(grid_f32, grid_f32, grid_f32, gri...  5.62 us
    pallas_call x1, Pallas kernels, body(): pl.pallas_call(functools.partial(step_kernel, True), out_shape=(grid_f32,...  4.13 us
    all_to_all x1, starting transfers between devices, exchange(): return lax.all_to_all(pay, 'tm', 0, 0)  3.55 us
    pallas_call x1, Pallas kernels, body(): pl.pallas_call(first_step_kernel, out_shape=(grid_f32, grid_f32, grid_f32...  3.17 us
  transfers between devices with their start and end apart: 1, of which 1 were waited for; matrix products, arithmetic and copies ran while one was open for 0% of the time, Pallas kernels for 2%

profile of v2, /device:TPU:0, one launch (start us, length us, event | category | flops | bytes accessed | tf_op | source)
XLA Modules:
  0.0 69.2 jit_solution(14457268198105373789)
XLA Ops:
  0.6 0.0 copy-start.1
  0.6 0.0 copy-start
  0.7 5.6 %start.1 = (f32[64,2048]{1,0:T(8,128)S(1)}, f32[64,2048]{1,0:T(8,128)S(1)}, f32[64,2048]{1,0:T(8,128)S(1)}, f32[64,2048]{1,0:T(8,128)S(1)}, f32[1,2048]{1,0:T(1,128)S(1)}, /*index=5*/f32[16,32,128]{2,1,0:T(8,128)S(1)}) custom-call(s32[1]{0:T(128)} %bitcast.me_ref.me, bf16[64,2048]{1,0:T(8,128)(2,1)} %gate_hbm.1, bf16[64,2048]{1,0:T(8,128)(2,1)} %cand_hbm.1, ...), custom_call_target="tpu_custom_call" | custom-call | tf_op jit(solution)/shard_map/start/pallas_call | solution.py:344
  6.3 15.5 %all_to_all.20.got = f32[16,32,128]{2,1,0:T(8,128)S(1)} all-to-all(f32[16,32,128]{2,1,0:T(8,128)S(1)} %get-tuple-element.19), channel_id=1, replica_groups=mesh['tm'=16,'batch'=2] {'tm'}, dimensions={0} | all-to-all | bytes 524288 | tf_op jit(solution)/shard_map/all_to_all | solution.py:325
  21.7 0.0 copy-done.1
  21.7 0.0 copy-done
  21.7 3.2 %middle.1 = (f32[64,2048]{1,0:T(8,128)S(1)}, f32[64,2048]{1,0:T(8,128)S(1)}, f32[64,2048]{1,0:T(8,128)S(1)}, f32[8,128]{1,0:T(8,128)S(1)}, f32[16,32,128]{2,1,0:T(8,128)S(1)}) custom-call(s32[1]{0:T(128)} %bitcast.me_ref.me, f32[16,32,128]{2,1,0:T(8,128)S(1)} %all_to_all.20.got, f32[16,128]{1,0:T(8,128)S(1)} %bitcast.5, ...), custom_call_target="tpu_custom_call" | custom-call | tf_op jit(solution)/shard_map/middle/pallas_call | solution.py:374
  24.9 12.7 %all_to_all.21.got_ref = f32[16,32,128]{2,1,0:T(8,128)S(1)} all-to-all(f32[16,32,128]{2,1,0:T(8,128)S(1)} %get-tuple-element.25), channel_id=1, replica_groups=mesh['tm'=16,'batch'=2] {'tm'}, dimensions={0} | all-to-all | bytes 524288 | tf_op jit(solution)/shard_map/all_to_all | solution.py:325
  37.6 4.1 %last.1 = (f32[64,2048]{1,0:T(8,128)S(1)}, f32[64,2048]{1,0:T(8,128)S(1)}, f32[16,32,128]{2,1,0:T(8,128)S(1)}, f32[16,40,128]{2,1,0:T(8,128)}) custom-call(s32[1]{0:T(128)} %bitcast.me_ref.me, f32[16,32,128]{2,1,0:T(8,128)S(1)} %all_to_all.21.got_ref, f32[16,128]{1,0:T(8,128)S(1)} %bitcast.6, f32[64,2048]{1,0:T(8,128)S(1)} %get-tuple-element.20.keep.keep_ref, ...), custom_call_target="tpu_custom_call" | custom-call | tf_op jit(solution)/shard_map/last/pallas_call | solution.py:385
  41.7 12.6 %all_to_all.22.got_ref = f32[16,32,128]{2,1,0:T(8,128)S(1)} all-to-all(f32[16,32,128]{2,1,0:T(8,128)S(1)} %get-tuple-element.30), channel_id=1, replica_groups=mesh['tm'=16,'batch'=2] {'tm'}, dimensions={0} | all-to-all | bytes 524288 | tf_op jit(solution)/shard_map/all_to_all | solution.py:325
  54.3 3.5 %all-to-all-start.3 = ((f32[16,40,128]{2,1,0:T(8,128)}), f32[16,40,128]{2,1,0:T(8,128)S(1)}, u32[]{:S(2)}, u32[]{:S(2)}) async-start(f32[16,40,128]{2,1,0:T(8,128)} %get-tuple-element.35), calls=%async_computation.3 | async-start | bytes 655360 | tf_op jit(solution)/shard_map/all_to_all | solution.py:325
  57.9 1.2 %path.1 = (f32[64,2048]{1,0:T(8,128)}, f32[16,16,128]{2,1,0:T(8,128)S(1)}) custom-call(s32[1]{0:T(128)} %bitcast.me_ref.me, f32[16,32,128]{2,1,0:T(8,128)S(1)} %all_to_all.22.got_ref, f32[64,2048]{1,0:T(8,128)S(1)} %get-tuple-element.31.fresh_ref, f32[64,2048]{1,0:T(8,128)S(1)} %get-tuple-element.32.cum_a_ref), custom_call_target="tpu_custom_call" | custom-call | flops 10000000000 | bytes 2097152 | tf_op jit(solution)/shard_map/path/pallas_call | solution.py:402
  59.1 9.4 %all-to-all-done.3.sums_ref = f32[16,40,128]{2,1,0:T(8,128)S(1)} async-done(((f32[16,40,128]{2,1,0:T(8,128)}), f32[16,40,128]{2,1,0:T(8,128)S(1)}, u32[]{:S(2)}, u32[]{:S(2)}) %all-to-all-start.3) | async-done | bytes 327712 | tf_op jit(solution)/shard_map/all_to_all | solution.py:325
  68.5 0.8 %norm.1 = f32[3]{0:T(128)} custom-call(f32[16,16,128]{2,1,0:T(8,128)S(1)} %get-tuple-element.34.moves_ref, f32[16,40,128]{2,1,0:T(8,128)S(1)} %all-to-all-done.3.sums_ref), custom_call_target="tpu_custom_call" | custom-call | tf_op jit(solution)/shard_map/norm/pallas_call | solution.py:412
Async XLA Ops:
  0.6 21.1 %copy-start.1 = (f32[2048]{0:T(1024)S(1)}, f32[2048]{0:T(1024)}, u32[]{:S(2)}) copy-start(f32[2048]{0:T(1024)} %param.8) | copy-start | bytes 24580
  0.6 21.1 %copy-start = (bf16[2048,2048]{1,0:T(8,128)(2,1)S(1)}, bf16[2048,2048]{1,0:T(8,128)(2,1)}, u32[]{:S(2)}) copy-start(bf16[2048,2048]{1,0:T(8,128)(2,1)} %w_ref.1) | copy-start | bytes 25165828
  54.3 14.2 %all-to-all-start.3 = ((f32[16,40,128]{2,1,0:T(8,128)}), f32[16,40,128]{2,1,0:T(8,128)S(1)}, u32[]{:S(2)}, u32[]{:S(2)}) async-start(f32[16,40,128]{2,1,0:T(8,128)} %get-tuple-element.35), calls=%async_computation.3 | async-start | bytes 655360 | tf_op jit(solution)/shard_map/all_to_all | solution.py:325

commit v3 on v2

--- a/solution.py
+++ b/solution.py
@@ -17,7 +17,7 @@
 
 
 def softplus(x):
-    return jnp.maximum(x, 0.0) + jnp.log1p(jnp.exp(-jnp.abs(x)))
+    return jnp.maximum(x, 0.0) + jnp.log(1.0 + jnp.exp(-jnp.abs(x)))
 
 
 def chunk_scan(mul, add):
@@ -106,30 +106,9 @@
 
     mixed[...] = jnp.zeros_like(mixed)
     rates_copy.wait()
-    turn = [pl.ds(r, SUB, stride=steps) for r in range(steps)]
-    for k in range(PARTS):
-        gate_copies[k].wait()
-        cand_copies[k].wait()
-
-        @pl.loop(k * (part // LANE), (k + 1) * (part // LANE))
-        def _(j):
-            cols = pl.ds(pl.multiple_of(j * LANE, LANE), LANE)
-            gate_nat[j] = gate_ref[:, cols].astype(F32)
-            base_nat[j] = cand_ref[:, cols].astype(F32)
-            rate = rates_ref[:, cols]
-            for r in range(steps):
-                here = pl.ds(r * SUB, SUB)
-                gate = gate_nat[j, turn[r], :]
-                keep_ref[here, cols] = jnp.exp(-rate * softplus(gate) - jnp.maximum(gate - 8.0, 0.0))
-                base_ref[here, cols] = base_nat[j, turn[r], :]
-
+    init_copy.wait()
     for copy in diag_copies:
         copy.wait()
-    on_diag = lax.broadcasted_iota(jnp.int32, (LANE, LANE), 0) == lax.broadcasted_iota(jnp.int32, (LANE, LANE), 1)
-    for k in range(tiles):
-        block = blocks[k].astype(F32)
-        diag_ref[:, k * LANE : (k + 1) * LANE] = jnp.sum(jnp.where(on_diag, block, 0.0), axis=0, keepdims=True)
-    init_copy.wait()
 
     @pl.when(me == 0)
     def _():
@@ -144,32 +123,52 @@
     def _():
         init_ref[...] = jnp.zeros_like(init_ref)
 
-    @pl.loop(0, width // WIDE)
-    def _(j):
-        cols = pl.ds(pl.multiple_of(j * WIDE, WIDE), WIDE)
-        top = lax.broadcasted_iota(jnp.int32, (SUB, WIDE), 0) == 0
-        unit = diag_ref[:, cols]
-        mul, add = [], []
-        for r in range(steps):
-            here = pl.ds(r * SUB, SUB)
-            keep = keep_ref[here, cols]
-            left = 1.0 - keep
-            base = base_ref[here, cols]
-            cand = jnp.tanh(base + jnp.where(top, mixed[:, cols], 0.0) if r == 0 else base)
-            slope = keep + left * (1.0 - cand * cand) * unit
-            offset = left * cand
-            if r == 0:
-                prev = jnp.where(top, init_ref[:, cols], 0.0)
-                offset = (keep * prev + offset) - slope * prev
-            mul.append(slope)
-            add.append(offset)
-        cum_a, cum_b = chunk_scan(mul, add)
-        for r in range(steps):
-            here = pl.ds(r * SUB, SUB)
-            cum_a_ref[here, cols] = cum_a[r]
-            cum_b_ref[here, cols] = cum_b[r]
-        write_rows(one, 0, j * per, cum_a[-1][SUB - 1 :, :])
-        write_rows(one, tiles, j * per, cum_b[-1][SUB - 1 :, :])
+    turn = [pl.ds(r, SUB, stride=steps) for r in range(steps)]
+    for p in range(PARTS):
+        gate_copies[p].wait()
+        cand_copies[p].wait()
+
+        @pl.loop(p * (part // WIDE), (p + 1) * (part // WIDE))
+        def _(j):
+            cols = pl.ds(pl.multiple_of(j * WIDE, WIDE), WIDE)
+            on_diag = lax.broadcasted_iota(jnp.int32, (LANE, LANE), 0) == lax.broadcasted_iota(
+                jnp.int32, (LANE, LANE), 1
+            )
+            units = []
+            for k in range(per):
+                here = pl.ds(pl.multiple_of(j * WIDE + k * LANE, LANE), LANE)
+                gate_nat[j * per + k] = gate_ref[:, here].astype(F32)
+                base_nat[j * per + k] = cand_ref[:, here].astype(F32)
+                block = jnp.where(on_diag, blocks[j * per + k].astype(F32), 0.0)
+                units.append(jnp.sum(block, axis=0, keepdims=True))
+            unit = jnp.concatenate(units, axis=1)
+            diag_ref[:, cols] = unit
+            top = lax.broadcasted_iota(jnp.int32, (SUB, WIDE), 0) == 0
+            rate = rates_ref[:, cols]
+            mul, add = [], []
+            for r in range(steps):
+                here = pl.ds(r * SUB, SUB)
+                gate = jnp.concatenate([gate_nat[j * per + k, turn[r], :] for k in range(per)], axis=1)
+                base = jnp.concatenate([base_nat[j * per + k, turn[r], :] for k in range(per)], axis=1)
+                keep = jnp.exp(-rate * softplus(gate) - jnp.maximum(gate - 8.0, 0.0))
+                keep_ref[here, cols] = keep
+                base_ref[here, cols] = base
+                left = 1.0 - keep
+                cand = jnp.tanh(base + jnp.where(top, mixed[:, cols], 0.0) if r == 0 else base)
+                slope = keep + left * (1.0 - cand * cand) * unit
+                offset = left * cand
+                if r == 0:
+                    prev = jnp.where(top, init_ref[:, cols], 0.0)
+                    offset = (keep * prev + offset) - slope * prev
+                mul.append(slope)
+                add.append(offset)
+            cum_a, cum_b = chunk_scan(mul, add)
+            for r in range(steps):
+                here = pl.ds(r * SUB, SUB)
+                cum_a_ref[here, cols] = cum_a[r]
+                cum_b_ref[here, cols] = cum_b[r]
+            write_rows(one, 0, j * per, cum_a[-1][SUB - 1 :, :])
+            write_rows(one, tiles, j * per, cum_b[-1][SUB - 1 :, :])
 
     spread(one, pay_ref)
 
@@ -179,9 +178,9 @@
     *rest,
 ):
     if last:
-        fresh_ref, out_a_ref, pay_ref, sums_ref, prev, low, entry, one, acc, more = rest
+        fresh_ref, out_a_ref, one, prev, low, entry, acc, mix = rest
     else:
-        state_ref, out_a_ref, out_b_ref, sum_ref, pay_ref, prev, low, entry, one, acc = rest
+        state_ref, out_a_ref, out_b_ref, sum_ref, pay_ref, prev, low, entry, one, acc, mix = rest
     rows, width = keep_ref.shape
     steps = rows // SUB
     tiles = width // LANE
@@ -217,21 +216,24 @@
     if not last:
         sum_ref[...] = acc[...]
     else:
-        more[pl.ds(2 * tiles, SUB), :] = jnp.zeros((SUB, LANE), F32)
-        more[pl.ds(2 * tiles, 1), :] = jnp.sum(tot_ref[...], axis=0, keepdims=True)
-        more[pl.ds(2 * tiles + 1, 1), :] = jnp.sum(acc[...], axis=0, keepdims=True)
+        one[pl.ds(4 * tiles, SUB), :] = jnp.zeros((SUB, LANE), F32)
+        one[pl.ds(4 * tiles, 1), :] = jnp.sum(tot_ref[...], axis=0, keepdims=True)
+        one[pl.ds(4 * tiles + 1, 1), :] = jnp.sum(acc[...], axis=0, keepdims=True)
         acc[...] = jnp.zeros_like(acc)
 
-    def solve(j, _):
+    def multiply(j, slot):
         cols = pl.ds(pl.multiple_of(j * WIDE, WIDE), WIDE)
-        mixed = jnp.dot(low[...], w_ref[:, cols], preferred_element_type=F32)
+        mix[slot] = jnp.dot(low[...], w_ref[:, cols], preferred_element_type=F32)
+
+    def solve(j, slot):
+        cols = pl.ds(pl.multiple_of(j * WIDE, WIDE), WIDE)
         unit = diag_ref[:, cols]
         mul, add = [], []
         for r in range(steps):
             here = pl.ds(r * SUB, SUB)
             keep = keep_ref[here, cols]
             before = prev[here, cols]
-            cand = jnp.tanh(base_ref[here, cols] + mixed[r * SUB : (r + 1) * SUB, :])
+            cand = jnp.tanh(base_ref[here, cols] + mix[slot, here, :])
             left = 1.0 - keep
             mapped = keep * before + left * cand
             slope = keep + left * (1.0 - cand * cand) * unit
@@ -249,16 +251,18 @@
                 else:
                     state = cum_b_ref[here, cols] + cum_a_ref[here, cols] * e
                 u = fresh - state
-                fresh_ref[here, cols] = fresh
-                out_a_ref[here, cols] = cum_a[r]
+                for k in range(per):
+                    part = slice(k * LANE, (k + 1) * LANE)
+                    fresh_ref[j * per + k, pl.ds(r, SUB, stride=steps), :] = fresh[:, part]
+                    out_a_ref[j * per + k, pl.ds(r, SUB, stride=steps), :] = cum_a[r][:, part]
                 c0 = c0 + u * u
                 c1 = c1 + u * cum_a[r]
                 c2 = c2 + cum_a[r] * cum_a[r]
             acc[...] += sum(c0[:, k * LANE : (k + 1) * LANE] for k in range(per))
             write_rows(one, 0, j * per, cum_a[-1][SUB - 1 :, :])
             write_rows(one, tiles, j * per, u[SUB - 1 :, :])
-            write_rows(more, 0, j * per, 2.0 * jnp.sum(c1, axis=0, keepdims=True))
-            write_rows(more, tiles, j * per, jnp.sum(c2, axis=0, keepdims=True))
+            write_rows(one, 2 * tiles, j * per, 2.0 * jnp.sum(c1, axis=0, keepdims=True))
+            write_rows(one, 3 * tiles, j * per, jnp.sum(c2, axis=0, keepdims=True))
         else:
             for r in range(steps):
                 here = pl.ds(r * SUB, SUB)
@@ -266,63 +270,94 @@
                 out_b_ref[here, cols] = cum_b[r]
             write_rows(one, 0, j * per, cum_a[-1][SUB - 1 :, :])
             write_rows(one, tiles, j * per, cum_b[-1][SUB - 1 :, :])
-        return 0
-
-    lax.fori_loop(0, width // WIDE, solve, 0)
+
+    blocks = width // WIDE
+    multiply(0, 0)
+
+    @pl.loop(0, blocks // 2 - 1)
+    def _(i):
+        multiply(2 * i + 1, 1)
+        solve(2 * i, 0)
+        multiply(2 * i + 2, 0)
+        solve(2 * i + 1, 1)
+
+    multiply(blocks - 1, 1)
+    solve(blocks - 2, 0)
+    solve(blocks - 1, 1)
     if last:
-        more[pl.ds(2 * tiles + 2, 1), :] = jnp.sum(acc[...], axis=0, keepdims=True)
-        spread(more, sums_ref)
-    spread(one, pay_ref)
+        one[pl.ds(4 * tiles + 2, 1), :] = jnp.sum(acc[...], axis=0, keepdims=True)
+    else:
+        spread(one, pay_ref)
 
 
 def first_step_kernel(me, got, init, keep, base, cum_a, cum_b, diag, w, *rest):
     step_kernel(False, me, got, init, keep, base, cum_a, cum_b, diag, w, None, None, *rest)
 
 
-def path_kernel(me_ref, got_ref, fresh_ref, cum_a_ref, path_ref, moves_ref, nat):
-    rows, width = fresh_ref.shape
-    steps = rows // SUB
-    tiles = width // LANE
-    peers = got_ref.shape[0]
-    moves_ref[0] = jnp.zeros((tiles, LANE), F32)
-
-    def pull(q, d):
-        d = got_ref[q, 0:tiles, :] * d + got_ref[q, tiles : 2 * tiles, :]
-        moves_ref[q + 1] = d
-        return d
-
-    lax.fori_loop(0, peers - 1, pull, moves_ref[0])
-
-    @pl.loop(0, tiles)
-    def _(j):
-        cols = pl.ds(pl.multiple_of(j * LANE, LANE), LANE)
-        e = moves_ref[me_ref[0], pl.ds(j, 1), :]
-        for r in range(steps):
-            here = pl.ds(r * SUB, SUB)
-            nat[j, pl.ds(r, SUB, stride=steps), :] = fresh_ref[here, cols] + cum_a_ref[here, cols] * e
-        path_ref[:, cols] = nat[j]
-
-
-def norm_kernel(count, moves_ref, sums_ref, norm_ref, quad_ref):
-    peers, tiles, _ = moves_ref.shape
+def pair_kernel(me_ref, one_ref, other_ref, pay_ref, both):
+    tiles = (one_ref.shape[0] - SUB) // 4
+
+    def join(first, second):
+        a1, b1, l1, q1 = (first[k * tiles : (k + 1) * tiles, :] for k in range(4))
+        a2, b2, l2, q2 = (second[k * tiles : (k + 1) * tiles, :] for k in range(4))
+        both[0:tiles, :] = a1 * a2
+        both[tiles : 2 * tiles, :] = a2 * b1 + b2
+        both[2 * tiles : 3 * tiles, :] = l1 + a1 * (l2 + 2.0 * q2 * b1)
+        both[3 * tiles : 4 * tiles, :] = q1 + a1 * a1 * q2
+        both[4 * tiles :, :] = first[4 * tiles :, :] + second[4 * tiles :, :]
+        extra = jnp.sum(b1 * (l2 + q2 * b1), axis=0, keepdims=True)
+        both[4 * tiles + 2 : 4 * tiles + 3, :] = both[4 * tiles + 2 : 4 * tiles + 3, :] + extra
+
+    @pl.when(lax.rem(me_ref[0], 2) == 0)
+    def _():
+        join(one_ref, other_ref)
+
+    @pl.when(lax.rem(me_ref[0], 2) == 1)
+    def _():
+        join(other_ref, one_ref)
+
+    spread(both, pay_ref)
+
+
+def final_kernel(count, me_ref, got_ref, other_ref, fresh_ref, cum_a_ref, path_ref, norm_ref, entry, quad_ref):
+    tiles = fresh_ref.shape[0]
+    pairs = got_ref.shape[0]
     quad_ref[...] = jnp.zeros_like(quad_ref)
-
-    def gather(q, carry):
-        quad, sums = carry
-        d = moves_ref[q]
-        quad = quad + d * (sums_ref[q, 0:tiles, :] + sums_ref[q, tiles : 2 * tiles, :] * d)
-        return quad, sums + sums_ref[q, 2 * tiles : 2 * tiles + SUB, :]
-
-    quad, sums = lax.fori_loop(0, peers, gather, (quad_ref[0:tiles, :], quad_ref[tiles:, :]))
+    pair = lax.div(me_ref[0], 2)
+
+    def pull(q, carry):
+        d, quad, sums = carry
+
+        @pl.when(q == pair)
+        def _():
+            entry[...] = d
+
+        quad = quad + d * (got_ref[q, 2 * tiles : 3 * tiles, :] + got_ref[q, 3 * tiles : 4 * tiles, :] * d)
+        sums = sums + got_ref[q, 4 * tiles : 4 * tiles + SUB, :]
+        return got_ref[q, 0:tiles, :] * d + got_ref[q, tiles : 2 * tiles, :], quad, sums
+
+    _, quad, sums = lax.fori_loop(
+        0, pairs, pull, (quad_ref[0:tiles, :], quad_ref[0:tiles, :], quad_ref[tiles:, :])
+    )
+
+    @pl.when(lax.rem(me_ref[0], 2) == 1)
+    def _():
+        entry[...] = other_ref[0:tiles, :] * entry[...] + other_ref[tiles : 2 * tiles, :]
+
     extra = jnp.sum(quad, axis=0, keepdims=True)
     totals = [sums[0:1, :], sums[1:2, :], sums[2:3, :] + extra]
     for k, row in enumerate(totals):
         total = jnp.sum(row, axis=1, keepdims=True)
         norm_ref[k] = jnp.max(jnp.sqrt(total / count))
 
-
-def exchange(pay):
-    return lax.all_to_all(pay, "tm", 0, 0)
+    @pl.loop(0, tiles)
+    def _(j):
+        cols = pl.ds(pl.multiple_of(j * LANE, LANE), LANE)
+        path_ref[:, cols] = fresh_ref[j] + cum_a_ref[j] * entry[pl.ds(j, 1), :]
+
+
+def exchange(pay, groups=None):
+    return lax.all_to_all(pay, "tm", 0, 0, axis_index_groups=groups)
 
 
 def body(gate_in, cand_in, rates, init_state, recur_weight):
@@ -330,7 +365,7 @@
     peers = lax.axis_size("tm")
     tiles = width // LANE
     steps = rows // SUB
-    assert rows % (2 * SUB) == 0 and width % WIDE == 0
+    assert rows % (2 * SUB) == 0 and width % (2 * WIDE) == 0 and peers % 2 == 0
     me = lax.axis_index("tm").astype(jnp.int32).reshape(1)
     init_row = init_state.reshape(1, width)
     init_tile = init_state.reshape(tiles, LANE)
@@ -339,7 +374,9 @@
     hbm = pl.BlockSpec(memory_space=pltpu.HBM)
     grid_f32 = jax.ShapeDtypeStruct((rows, width), F32)
     pay2 = jax.ShapeDtypeStruct((peers, 2 * tiles, LANE), F32)
-    pay3 = jax.ShapeDtypeStruct((peers, 2 * tiles + SUB, LANE), F32)
+    last1 = jax.ShapeDtypeStruct((4 * tiles + SUB, LANE), F32)
+    last8 = jax.ShapeDtypeStruct((peers // 2, 4 * tiles + SUB, LANE), F32)
+    turned = jax.ShapeDtypeStruct((tiles, rows, LANE), F32)
 
     keep, base, cum_a, cum_b, diag, pay = pl.pallas_call(
         start_kernel,
@@ -371,53 +408,49 @@
         pltpu.VMEM((rows, width), BF16),
         pltpu.VMEM((tiles, LANE), F32),
     ]
+    tail = [pltpu.VMEM((SUB, LANE), F32), pltpu.VMEM((2, rows, WIDE), F32)]
     state, cum_a, cum_b, moved, pay = pl.pallas_call(
         first_step_kernel,
         out_shape=(grid_f32, grid_f32, grid_f32, jax.ShapeDtypeStruct((SUB, LANE), F32), pay2),
         in_specs=[smem] + [vmem] * 8,
         out_specs=(vmem,) * 5,
-        scratch_shapes=scratch + [pltpu.VMEM((2 * tiles, LANE), F32), pltpu.VMEM((SUB, LANE), F32)],
+        scratch_shapes=scratch + [pltpu.VMEM((2 * tiles, LANE), F32)] + tail,
         compiler_params=pltpu.CompilerParams(vmem_limit_bytes=VMEM_LIMIT),
         name="middle",
     )(me, got, init_tile, keep, base, cum_a, cum_b, diag, recur_weight)
     got = exchange(pay)
 
-    fresh, cum_a, pay, sums = pl.pallas_call(
+    fresh, cum_a, one = pl.pallas_call(
         functools.partial(step_kernel, True),
-        out_shape=(grid_f32, grid_f32, pay2, pay3),
+        out_shape=(turned, turned, last1),
         in_specs=[smem] + [vmem] * 10,
-        out_specs=(vmem,) * 4,
-        scratch_shapes=scratch
-        + [
-            pltpu.VMEM((2 * tiles, LANE), F32),
-            pltpu.VMEM((SUB, LANE), F32),
-            pltpu.VMEM((2 * tiles + SUB, LANE), F32),
-        ],
+        out_specs=(vmem,) * 3,
+        scratch_shapes=scratch + tail,
         compiler_params=pltpu.CompilerParams(vmem_limit_bytes=VMEM_LIMIT),
         name="last",
     )(me, got, init_tile, keep, base, cum_a, cum_b, diag, recur_weight, state, moved)
-    got = exchange(pay)
-    sums = exchange(sums)
-
-    path, moves = pl.pallas_call(
-        path_kernel,
-        out_shape=(grid_f32, jax.ShapeDtypeStruct((peers, tiles, LANE), F32)),
-        in_specs=[smem] + [vmem] * 3,
-        out_specs=(vmem,) * 2,
-        scratch_shapes=[pltpu.VMEM((tiles, rows, LANE), F32)],
+
+    other = lax.ppermute(one, "tm", [(k, k ^ 1) for k in range(peers)])
+    pay = pl.pallas_call(
+        pair_kernel,
+        out_shape=last8,
+        in_specs=[smem] + [vmem] * 2,
+        out_specs=vmem,
+        scratch_shapes=[pltpu.VMEM(last1.shape, F32)],
         compiler_params=pltpu.CompilerParams(vmem_limit_bytes=VMEM_LIMIT),
-        cost_estimate=pl.CostEstimate(flops=10**10, bytes_accessed=2**21, transcendentals=0),
-        name="path",
-    )(me, got, fresh, cum_a)
-    norms = pl.pallas_call(
-        functools.partial(norm_kernel, peers * rows * width),
-        out_shape=jax.ShapeDtypeStruct((3,), F32),
-        in_specs=[vmem] * 2,
-        out_specs=smem,
-        scratch_shapes=[pltpu.VMEM((tiles + SUB, LANE), F32)],
+        name="pair",
+    )(me, one, other)
+    got = exchange(pay, [[2 * k + s for k in range(peers // 2)] for s in range(2)])
+
+    path, norms = pl.pallas_call(
+        functools.partial(final_kernel, peers * rows * width),
+        out_shape=(grid_f32, jax.ShapeDtypeStruct((3,), F32)),
+        in_specs=[smem] + [vmem] * 4,
+        out_specs=(vmem, smem),
+        scratch_shapes=[pltpu.VMEM((tiles, LANE), F32), pltpu.VMEM((tiles + SUB, LANE), F32)],
         compiler_params=pltpu.CompilerParams(vmem_limit_bytes=VMEM_LIMIT),
-        name="norm",
-    )(moves, sums)
+        name="final",
+    )(me, got, other, fresh, cum_a)
     return path, norms
 
 

time: 69.5 us -> 56.9 us (0.82)
  waiting for transfers between devices: 9.37 us -> 3.18 us
  starting transfers between devices: 3.55 us -> 0.84 us
  Pallas kernels: 14.9 us -> 12.5 us
  blocking collectives: 40.7 us -> 39.4 us
    all_to_all x1 -> x0, waiting for transfers between devices: 9.37 us -> none  [exchange(): return lax.all_to_all(pay, 'tm', 0, 0)]
    all_to_all x1 -> x0, starting transfers between devices: 3.55 us -> none  [exchange(): return lax.all_to_all(pay, 'tm', 0, 0)]
    ppermute x0 -> x1, waiting for transfers between devices: none -> 3.18 us  [body(): other = lax.ppermute(one, 'tm', [(k, k ^ 1) for k in range(peers)])]
    pallas_call x3, Pallas kernels: 6.11 us -> 3.85 us  [the longest x1 2.67 us: body(): pl.pallas_call(functools.partial(step_kernel, True), out_shape=(turned, t...]
    all_to_all x3, blocking collectives: 40.7 us -> 39.4 us  [exchange(): return lax.all_to_all(pay, 'tm', 0, 0, axis_index_groups=groups)]
    ppermute x0 -> x1, starting transfers between devices: none -> 0.84 us  [body(): other = lax.ppermute(one, 'tm', [(k, k ^ 1) for k in range(peers)])]
  transfers between devices with their start and end apart: 1 -> 1, of which waited for: 1 -> 1; matrix products, arithmetic and copies ran while one was open for 0% -> 0% of each run, Pallas kernels for 2% -> 0%
where the time goes in v3:
time: 56.9 us; the launch traced here: 56.6 us
  blocking collectives  39.4 us (69%)
  Pallas kernels  12.5 us (22%)
  waiting for transfers between devices  3.18 us (6%)
  starting transfers between devices  0.84 us (1%)
  between operations  0.68 us (1%)
    all_to_all x3, blocking collectives, exchange(): return lax.all_to_all(pay, 'tm', 0, 0, axis_index_groups=groups)  39.4 us
    pallas_call x1, Pallas kernels, body(): pl.pallas_call(start_kernel, out_shape=(grid_f32, grid_f32, grid_f32, gri...  6.17 us
    ppermute x1, waiting for transfers between devices, body(): other = lax.ppermute(one, 'tm', [(k, k ^ 1) for k in range(peers)])  3.18 us
    pallas_call x1, Pallas kernels, body(): pl.pallas_call(functools.partial(step_kernel, True), out_shape=(turned, t...  2.67 us
    pallas_call x1, Pallas kernels, body(): pl.pallas_call(first_step_kernel, out_shape=(grid_f32, grid_f32, grid_f32...  2.51 us
    pallas_call x1, Pallas kernels, body(): pl.pallas_call(functools.partial(final_kernel, peers * rows * width), out...  1.14 us
  transfers between devices with their start and end apart: 1, of which 1 were waited for; matrix products, arithmetic and copies ran while one was open for 0% of the time, Pallas kernels for 0%

profile of v3, /device:TPU:0, one launch (start us, length us, event | category | flops | bytes accessed | tf_op | source)
XLA Modules:
  0.0 56.6 jit_solution(16032673352109249509)
XLA Ops:
  0.6 0.0 copy-start.1
  0.6 0.0 copy-start
  0.7 6.2 %start.1 = (f32[64,2048]{1,0:T(8,128)S(1)}, f32[64,2048]{1,0:T(8,128)S(1)}, f32[64,2048]{1,0:T(8,128)S(1)}, f32[64,2048]{1,0:T(8,128)S(1)}, f32[1,2048]{1,0:T(1,128)S(1)}, /*index=5*/f32[16,32,128]{2,1,0:T(8,128)S(1)}) custom-call(s32[1]{0:T(128)} %bitcast.me_ref.me, bf16[64,2048]{1,0:T(8,128)(2,1)} %gate_hbm.1, bf16[64,2048]{1,0:T(8,128)(2,1)} %cand_hbm.1, ...), custom_call_target="tpu_custom_call" | custom-call | tf_op jit(solution)/shard_map/start/pallas_call | solution.py:381
  6.8 14.6 %all_to_all.15.got = f32[16,32,128]{2,1,0:T(8,128)S(1)} all-to-all(f32[16,32,128]{2,1,0:T(8,128)S(1)} %get-tuple-element.16), channel_id=1, replica_groups=mesh['tm'=16,'batch'=2] {'tm'}, dimensions={0} | all-to-all | bytes 524288 | tf_op jit(solution)/shard_map/all_to_all | solution.py:360
  21.5 0.0 copy-done.1
  21.5 0.0 copy-done
  21.5 2.5 %middle.1 = (f32[64,2048]{1,0:T(8,128)S(1)}, f32[64,2048]{1,0:T(8,128)S(1)}, f32[64,2048]{1,0:T(8,128)S(1)}, f32[8,128]{1,0:T(8,128)S(1)}, f32[16,32,128]{2,1,0:T(8,128)S(1)}) custom-call(s32[1]{0:T(128)} %bitcast.me_ref.me, f32[16,32,128]{2,1,0:T(8,128)S(1)} %all_to_all.15.got, f32[16,128]{1,0:T(8,128)S(1)} %bitcast.5, ...), custom_call_target="tpu_custom_call" | custom-call | tf_op jit(solution)/shard_map/middle/pallas_call | solution.py:412
  24.0 12.7 %all_to_all.16.got_ref = f32[16,32,128]{2,1,0:T(8,128)S(1)} all-to-all(f32[16,32,128]{2,1,0:T(8,128)S(1)} %get-tuple-element.22), channel_id=1, replica_groups=mesh['tm'=16,'batch'=2] {'tm'}, dimensions={0} | all-to-all | bytes 524288 | tf_op jit(solution)/shard_map/all_to_all | solution.py:360
  36.7 2.7 %last.1 = (f32[16,64,128]{2,1,0:T(8,128)S(1)}, f32[16,64,128]{2,1,0:T(8,128)S(1)}, f32[72,128]{1,0:T(8,128)S(1)}) custom-call(s32[1]{0:T(128)} %bitcast.me_ref.me, f32[16,32,128]{2,1,0:T(8,128)S(1)} %all_to_all.16.got_ref, f32[16,128]{1,0:T(8,128)S(1)} %bitcast.6, f32[64,2048]{1,0:T(8,128)S(1)} %get-tuple-element.17.keep.keep_ref, ...), custom_call_target="tpu_custom_call" | custom-call | tf_op jit(solution)/shard_map/last/pallas_call | solution.py:423
  39.3 0.8 %collective-permute-start = (f32[72,128]{1,0:T(8,128)S(1)}, f32[72,128]{1,0:T(8,128)S(1)}, u32[]{:S(2)}, u32[]{:S(2)}) collective-permute-start(f32[72,128]{1,0:T(8,128)S(1)} %get-tuple-element.27.one_ref), channel_id=1, source_target_pairs={{0,2},{2,0},{4,6},{6,4},{8,10},{10,8},{12,14},{14,12},{16,18},{18,... | collective-permute-start | bytes 110600 | tf_op jit(solution)/shard_map/ppermute | solution.py:433
  40.2 3.2 %collective-permute-done.other_ref = f32[72,128]{1,0:T(8,128)S(1)} collective-permute-done((f32[72,128]{1,0:T(8,128)S(1)}, f32[72,128]{1,0:T(8,128)S(1)}, u32[]{:S(2)}, u32[]{:S(2)}) %collective-permute-start) | collective-permute-done | bytes 36896 | tf_op jit(solution)/shard_map/ppermute | solution.py:433
  43.4 12.1 %all_to_all.17.got_ref = f32[8,72,128]{2,1,0:T(8,128)S(1)} all-to-all(f32[8,72,128]{2,1,0:T(8,128)S(1)} %pair.1), channel_id=1, replica_groups={{0,4,8,12,16,20,24,28},{2,6,10,14,18,22,26,30},{1,5,9,13,17,21,25,29},{..., dimensions={0} | all-to-all | bytes 589824 | tf_op jit(solution)/shard_map/all_to_all | solution.py:360
  55.5 1.1 %final.1 = (f32[64,2048]{1,0:T(8,128)}, f32[3]{0:T(128)}) custom-call(s32[1]{0:T(128)} %bitcast.me_ref.me, f32[8,72,128]{2,1,0:T(8,128)S(1)} %all_to_all.17.got_ref, f32[72,128]{1,0:T(8,128)S(1)} %collective-permute-done.other_ref, f32[16,64,128]{2,1,0:T(8,128)S(1)} %get-tuple-element.28.fresh_ref, f32[16,64,128]{2,1,0:T(8,128)S(1)} %get-tuple-element.29.cum_a_ref), custom_call_target="tpu_custom_call" | custom-call | tf_op jit(solution)/shard_map/final/pallas_call | solution.py:445
  (1 shorter events, 0.0 us)
Async XLA Ops:
  0.6 20.8 %copy-start.1 = (f32[2048]{0:T(1024)S(1)}, f32[2048]{0:T(1024)}, u32[]{:S(2)}) copy-start(f32[2048]{0:T(1024)} %param.8) | copy-start | bytes 24580
  0.6 20.8 %copy-start = (bf16[2048,2048]{1,0:T(8,128)(2,1)S(1)}, bf16[2048,2048]{1,0:T(8,128)(2,1)}, u32[]{:S(2)}) copy-start(bf16[2048,2048]{1,0:T(8,128)(2,1)} %w_ref.1) | copy-start | bytes 25165828
  39.3 4.0 %collective-permute-start = (f32[72,128]{1,0:T(8,128)S(1)}, f32[72,128]{1,0:T(8,128)S(1)}, u32[]{:S(2)}, u32[]{:S(2)}) collective-permute-start(f32[72,128]{1,0:T(8,128)S(1)} %get-tuple-element.27.one_ref), channel_id=1, source_target_pairs={{0,2},{2,0},{4,6},{6,4},{8,10},{10,8},{12,14},{14,12},{16,18},{18,... | collective-permute-start | bytes 110600 | tf_op jit(solution)/shard_map/ppermute | solution.py:433

commit v4 on v3

--- a/solution.py
+++ b/solution.py
@@ -10,14 +10,19 @@
 SUB = 8
 LANE = 128
 WIDE = 256
-PARTS = 4
+PARTS = 2
+CHUNKS = 2
 VMEM_LIMIT = 16 * 1024 * 1024
 F32 = jnp.float32
 BF16 = jnp.bfloat16
 
 
-def softplus(x):
-    return jnp.maximum(x, 0.0) + jnp.log(1.0 + jnp.exp(-jnp.abs(x)))
+LOG2E = 1.4426950408889634
+
+
+def keep_of(gate, rate2):
+    soft = jnp.maximum(gate, 0.0) + jnp.log(1.0 + jnp.exp2(jnp.abs(gate) * -LOG2E))
+    return jnp.exp2(-rate2 * soft - jnp.maximum(gate * LOG2E - 8.0 * LOG2E, 0.0))
 
 
 def chunk_scan(mul, add):
@@ -91,10 +96,10 @@
         )
         for k in range(PARTS)
     ]
-    rates_copy.start()
     for k in range(PARTS):
         gate_copies[k].start()
         cand_copies[k].start()
+    rates_copy.start()
     init_copy.start()
     for copy in diag_copies:
         copy.start()
@@ -128,7 +133,7 @@
         gate_copies[p].wait()
         cand_copies[p].wait()
 
-        @pl.loop(p * (part // WIDE), (p + 1) * (part // WIDE))
+        @pl.loop(p * (part // WIDE), (p + 1) * (part // WIDE), unroll=True)
         def _(j):
             cols = pl.ds(pl.multiple_of(j * WIDE, WIDE), WIDE)
             on_diag = lax.broadcasted_iota(jnp.int32, (LANE, LANE), 0) == lax.broadcasted_iota(
@@ -144,13 +149,13 @@
             unit = jnp.concatenate(units, axis=1)
             diag_ref[:, cols] = unit
             top = lax.broadcasted_iota(jnp.int32, (SUB, WIDE), 0) == 0
-            rate = rates_ref[:, cols]
+            rate = rates_ref[:, cols] * LOG2E
             mul, add = [], []
             for r in range(steps):
                 here = pl.ds(r * SUB, SUB)
                 gate = jnp.concatenate([gate_nat[j * per + k, turn[r], :] for k in range(per)], axis=1)
                 base = jnp.concatenate([base_nat[j * per + k, turn[r], :] for k in range(per)], axis=1)
-                keep = jnp.exp(-rate * softplus(gate) - jnp.maximum(gate - 8.0, 0.0))
+                keep = keep_of(gate, rate)
                 keep_ref[here, cols] = keep
                 base_ref[here, cols] = base
                 left = 1.0 - keep
@@ -192,8 +197,8 @@
     entry[...] = lax.fori_loop(0, me_ref[0], pull, init_ref[...])
     acc[...] = jnp.zeros_like(acc)
 
-    def turned_state(j, _):
-        cols = pl.ds(pl.multiple_of(j * WIDE, WIDE), WIDE)
+    def turned_state(j):
+        cols = slice(j * WIDE, (j + 1) * WIDE)
         e = read_row(entry, j * per, per)
         state = [
             cum_b_ref[pl.ds(r * SUB, SUB), cols] + cum_a_ref[pl.ds(r * SUB, SUB), cols] * e for r in range(steps)
@@ -207,12 +212,12 @@
             moved = moved + change * change
             if not last:
                 state_ref[pl.ds(r * SUB, SUB), cols] = state[r]
-        for r in range(0, steps, 2):
-            low[pl.ds(r * SUB, 2 * SUB), cols] = jnp.concatenate(before[r : r + 2], axis=0).astype(BF16)
+        rounded = jnp.concatenate(before, axis=0).astype(BF16)
+        low[:, cols] = rounded
         acc[...] += sum(moved[:, k * LANE : (k + 1) * LANE] for k in range(per))
-        return 0
-
-    lax.fori_loop(0, width // WIDE, turned_state, 0)
+        return jnp.dot(rounded, w_ref[cols, 0:WIDE], preferred_element_type=F32)
+
+    mix[0] = sum(turned_state(j) for j in range(width // WIDE))
     if not last:
         sum_ref[...] = acc[...]
     else:
@@ -272,9 +277,8 @@
             write_rows(one, tiles, j * per, cum_b[-1][SUB - 1 :, :])
 
     blocks = width // WIDE
-    multiply(0, 0)
-
-    @pl.loop(0, blocks // 2 - 1)
+
+    @pl.loop(0, blocks // 2 - 1, unroll=True)
     def _(i):
         multiply(2 * i + 1, 1)
         solve(2 * i, 0)
@@ -319,41 +323,49 @@
     spread(both, pay_ref)
 
 
-def final_kernel(count, me_ref, got_ref, other_ref, fresh_ref, cum_a_ref, path_ref, norm_ref, entry, quad_ref):
-    tiles = fresh_ref.shape[0]
+def final_kernel(
+    count, me_ref, got_ref, other_ref, fresh_ref, cum_a_ref, path_hbm, norm_hbm, moves, entry, path, norm_ref, sem
+):
+    tiles, rows, _ = fresh_ref.shape
     pairs = got_ref.shape[0]
-    quad_ref[...] = jnp.zeros_like(quad_ref)
-    pair = lax.div(me_ref[0], 2)
-
-    def pull(q, carry):
-        d, quad, sums = carry
-
-        @pl.when(q == pair)
-        def _():
-            entry[...] = d
-
+    moves[0] = jnp.zeros((tiles, LANE), F32)
+
+    def pull(q, d):
+        d = got_ref[q, 0:tiles, :] * d + got_ref[q, tiles : 2 * tiles, :]
+        moves[q + 1] = d
+        return d
+
+    lax.fori_loop(0, pairs - 1, pull, moves[0], unroll=True)
+    entry[...] = moves[lax.div(me_ref[0], 2)]
+
+    @pl.when(lax.rem(me_ref[0], 2) == 1)
+    def _():
+        entry[...] = other_ref[0:tiles, :] * entry[...] + other_ref[tiles : 2 * tiles, :]
+
+    copies = []
+    for p in range(CHUNKS):
+        for j in range(p * tiles // CHUNKS, (p + 1) * tiles // CHUNKS):
+            path[:, j * LANE : (j + 1) * LANE] = fresh_ref[j] + cum_a_ref[j] * entry[j : j + 1, :]
+        here = pl.ds(p * (tiles // CHUNKS) * LANE, (tiles // CHUNKS) * LANE)
+        copies.append(pltpu.make_async_copy(path.at[:, here], path_hbm.at[:, here], sem.at[p]))
+        copies[-1].start()
+
+    def gather(q, carry):
+        quad, sums = carry
+        d = moves[q]
         quad = quad + d * (got_ref[q, 2 * tiles : 3 * tiles, :] + got_ref[q, 3 * tiles : 4 * tiles, :] * d)
-        sums = sums + got_ref[q, 4 * tiles : 4 * tiles + SUB, :]
-        return got_ref[q, 0:tiles, :] * d + got_ref[q, tiles : 2 * tiles, :], quad, sums
-
-    _, quad, sums = lax.fori_loop(
-        0, pairs, pull, (quad_ref[0:tiles, :], quad_ref[0:tiles, :], quad_ref[tiles:, :])
-    )
-
-    @pl.when(lax.rem(me_ref[0], 2) == 1)
-    def _():
-        entry[...] = other_ref[0:tiles, :] * entry[...] + other_ref[tiles : 2 * tiles, :]
-
+        return quad, sums + got_ref[q, 4 * tiles : 4 * tiles + SUB, :]
+
+    quad, sums = lax.fori_loop(0, pairs, gather, (moves[0], moves[0, 0:SUB, :]), unroll=True)
     extra = jnp.sum(quad, axis=0, keepdims=True)
     totals = [sums[0:1, :], sums[1:2, :], sums[2:3, :] + extra]
     for k, row in enumerate(totals):
         total = jnp.sum(row, axis=1, keepdims=True)
         norm_ref[k] = jnp.max(jnp.sqrt(total / count))
-
-    @pl.loop(0, tiles)
-    def _(j):
-        cols = pl.ds(pl.multiple_of(j * LANE, LANE), LANE)
-        path_ref[:, cols] = fresh_ref[j] + cum_a_ref[j] * entry[pl.ds(j, 1), :]
+    copies.append(pltpu.make_async_copy(norm_ref, norm_hbm, sem.at[CHUNKS]))
+    copies[-1].start()
+    for copy in copies:
+        copy.wait()
 
 
 def exchange(pay, groups=None):
@@ -446,8 +458,14 @@
         functools.partial(final_kernel, peers * rows * width),
         out_shape=(grid_f32, jax.ShapeDtypeStruct((3,), F32)),
         in_specs=[smem] + [vmem] * 4,
-        out_specs=(vmem, smem),
-        scratch_shapes=[pltpu.VMEM((tiles, LANE), F32), pltpu.VMEM((tiles + SUB, LANE), F32)],
+        out_specs=(hbm, hbm),
+        scratch_shapes=[
+            pltpu.VMEM((peers // 2, tiles, LANE), F32),
+            pltpu.VMEM((tiles, LANE), F32),
+            pltpu.VMEM((rows, width), F32),
+            pltpu.SMEM((3,), F32),
+            pltpu.SemaphoreType.DMA((CHUNKS + 1,)),
+        ],
         compiler_params=pltpu.CompilerParams(vmem_limit_bytes=VMEM_LIMIT),
         name="final",
     )(me, got, other, fresh, cum_a)

time: 56.9 us -> 55.4 us (0.974)
  Pallas kernels: 12.5 us -> 11.4 us
where the time goes in v4:
time: 55.4 us; the launch traced here: 55.1 us
  blocking collectives  39 us (70%)
  Pallas kernels  11.4 us (21%)
  waiting for transfers between devices  3.19 us (6%)
  starting transfers between devices  0.84 us (2%)
  between operations  0.69 us (1%)
    all_to_all x3, blocking collectives, exchange(): return lax.all_to_all(pay, 'tm', 0, 0, axis_index_groups=groups)  39 us
    pallas_call x1, Pallas kernels, body(): pl.pallas_call(start_kernel, out_shape=(grid_f32, grid_f32, grid_f32, gri...  6.34 us
    ppermute x1, waiting for transfers between devices, body(): other = lax.ppermute(one, 'tm', [(k, k ^ 1) for k in range(peers)])  3.19 us
    pallas_call x1, Pallas kernels, body(): pl.pallas_call(functools.partial(step_kernel, True), out_shape=(turned, t...  2.18 us
    pallas_call x1, Pallas kernels, body(): pl.pallas_call(first_step_kernel, out_shape=(grid_f32, grid_f32, grid_f32...  1.98 us
  transfers between devices with their start and end apart: 1, of which 1 were waited for; matrix products, arithmetic and copies ran while one was open for 0% of the time, Pallas kernels for 0%

profile of v4, /device:TPU:0, one launch (start us, length us, event | category | flops | bytes accessed | tf_op | source)
XLA Modules:
  0.0 55.1 jit_solution(5411755727607569841)
XLA Ops:
  0.6 0.0 copy-start.1
  0.6 0.0 copy-start
  0.7 6.3 %start.1 = (f32[64,2048]{1,0:T(8,128)S(1)}, f32[64,2048]{1,0:T(8,128)S(1)}, f32[64,2048]{1,0:T(8,128)S(1)}, f32[64,2048]{1,0:T(8,128)S(1)}, f32[1,2048]{1,0:T(1,128)S(1)}, /*index=5*/f32[16,32,128]{2,1,0:T(8,128)S(1)}) custom-call(s32[1]{0:T(128)} %bitcast.me_ref.me, bf16[64,2048]{1,0:T(8,128)(2,1)} %gate_hbm.1, bf16[64,2048]{1,0:T(8,128)(2,1)} %cand_hbm.1, ...), custom_call_target="tpu_custom_call" | custom-call | tf_op jit(solution)/shard_map/start/pallas_call | solution.py:393
  7.0 14.2 %all_to_all.15.got = f32[16,32,128]{2,1,0:T(8,128)S(1)} all-to-all(f32[16,32,128]{2,1,0:T(8,128)S(1)} %get-tuple-element.16), channel_id=1, replica_groups=mesh['tm'=16,'batch'=2] {'tm'}, dimensions={0} | all-to-all | bytes 524288 | tf_op jit(solution)/shard_map/all_to_all | solution.py:372
  21.2 0.0 copy-done.1
  21.2 0.0 copy-done
  21.2 2.0 %middle.1 = (f32[64,2048]{1,0:T(8,128)S(1)}, f32[64,2048]{1,0:T(8,128)S(1)}, f32[64,2048]{1,0:T(8,128)S(1)}, f32[8,128]{1,0:T(8,128)S(1)}, f32[16,32,128]{2,1,0:T(8,128)S(1)}) custom-call(s32[1]{0:T(128)} %bitcast.me_ref.me, f32[16,32,128]{2,1,0:T(8,128)S(1)} %all_to_all.15.got, f32[16,128]{1,0:T(8,128)S(1)} %bitcast.5, ...), custom_call_target="tpu_custom_call" | custom-call | tf_op jit(solution)/shard_map/middle/pallas_call | solution.py:424
  23.2 12.7 %all_to_all.16.got_ref = f32[16,32,128]{2,1,0:T(8,128)S(1)} all-to-all(f32[16,32,128]{2,1,0:T(8,128)S(1)} %get-tuple-element.22), channel_id=1, replica_groups=mesh['tm'=16,'batch'=2] {'tm'}, dimensions={0} | all-to-all | bytes 524288 | tf_op jit(solution)/shard_map/all_to_all | solution.py:372
  35.9 2.2 %last.1 = (f32[16,64,128]{2,1,0:T(8,128)S(1)}, f32[16,64,128]{2,1,0:T(8,128)S(1)}, f32[72,128]{1,0:T(8,128)S(1)}) custom-call(s32[1]{0:T(128)} %bitcast.me_ref.me, f32[16,32,128]{2,1,0:T(8,128)S(1)} %all_to_all.16.got_ref, f32[16,128]{1,0:T(8,128)S(1)} %bitcast.6, f32[64,2048]{1,0:T(8,128)S(1)} %get-tuple-element.17.keep.keep_ref, ...), custom_call_target="tpu_custom_call" | custom-call | tf_op jit(solution)/shard_map/last/pallas_call | solution.py:435
  38.1 0.8 %collective-permute-start = (f32[72,128]{1,0:T(8,128)S(1)}, f32[72,128]{1,0:T(8,128)S(1)}, u32[]{:S(2)}, u32[]{:S(2)}) collective-permute-start(f32[72,128]{1,0:T(8,128)S(1)} %get-tuple-element.27.one_ref), channel_id=1, source_target_pairs={{0,2},{2,0},{4,6},{6,4},{8,10},{10,8},{12,14},{14,12},{16,18},{18,... | collective-permute-start | bytes 110600 | tf_op jit(solution)/shard_map/ppermute | solution.py:445
  38.9 3.2 %collective-permute-done.other_ref = f32[72,128]{1,0:T(8,128)S(1)} collective-permute-done((f32[72,128]{1,0:T(8,128)S(1)}, f32[72,128]{1,0:T(8,128)S(1)}, u32[]{:S(2)}, u32[]{:S(2)}) %collective-permute-start) | collective-permute-done | bytes 36896 | tf_op jit(solution)/shard_map/ppermute | solution.py:445
  42.2 12.1 %all_to_all.17.got_ref = f32[8,72,128]{2,1,0:T(8,128)S(1)} all-to-all(f32[8,72,128]{2,1,0:T(8,128)S(1)} %pair.1), channel_id=1, replica_groups={{0,4,8,12,16,20,24,28},{2,6,10,14,18,22,26,30},{1,5,9,13,17,21,25,29},{..., dimensions={0} | all-to-all | bytes 589824 | tf_op jit(solution)/shard_map/all_to_all | solution.py:372
  54.2 0.9 %final.1 = (f32[64,2048]{1,0:T(8,128)}, f32[3]{0:T(128)}) custom-call(s32[1]{0:T(128)} %bitcast.me_ref.me, f32[8,72,128]{2,1,0:T(8,128)S(1)} %all_to_all.17.got_ref, f32[72,128]{1,0:T(8,128)S(1)} %collective-permute-done.other_ref, f32[16,64,128]{2,1,0:T(8,128)S(1)} %get-tuple-element.28.fresh_ref, f32[16,64,128]{2,1,0:T(8,128)S(1)} %get-tuple-element.29.cum_a_ref), custom_call_target="tpu_custom_call" | custom-call | tf_op jit(solution)/shard_map/final/pallas_call | solution.py:457
  (1 shorter events, 0.0 us)
Async XLA Ops:
  0.6 20.6 %copy-start.1 = (f32[2048]{0:T(1024)S(1)}, f32[2048]{0:T(1024)}, u32[]{:S(2)}) copy-start(f32[2048]{0:T(1024)} %param.8) | copy-start | bytes 24580
  0.6 20.6 %copy-start = (bf16[2048,2048]{1,0:T(8,128)(2,1)S(1)}, bf16[2048,2048]{1,0:T(8,128)(2,1)}, u32[]{:S(2)}) copy-start(bf16[2048,2048]{1,0:T(8,128)(2,1)} %w_ref.1) | copy-start | bytes 25165828
  38.1 4.0 %collective-permute-start = (f32[72,128]{1,0:T(8,128)S(1)}, f32[72,128]{1,0:T(8,128)S(1)}, u32[]{:S(2)}, u32[]{:S(2)}) collective-permute-start(f32[72,128]{1,0:T(8,128)S(1)} %get-tuple-element.27.one_ref), channel_id=1, source_target_pairs={{0,2},{2,0},{4,6},{6,4},{8,10},{10,8},{12,14},{14,12},{16,18},{18,... | collective-permute-start | bytes 110600 | tf_op jit(solution)/shard_map/ppermute | solution.py:445

commit v5 on v4

--- a/solution.py
+++ b/solution.py
@@ -12,6 +12,10 @@
 WIDE = 256
 PARTS = 2
 CHUNKS = 2
+ORDERS = {
+    8: [4, 0, 7, 3, 1, 6, 5, 2],
+    16: [11, 5, 13, 14, 10, 8, 6, 0, 3, 1, 4, 2, 7, 9, 15, 12],
+}
 VMEM_LIMIT = 16 * 1024 * 1024
 F32 = jnp.float32
 BF16 = jnp.bfloat16
@@ -191,10 +195,12 @@
     tiles = width // LANE
     per = WIDE // LANE
 
-    def pull(q, e):
-        return got_ref[q, 0:tiles, :] * e + got_ref[q, tiles : 2 * tiles, :]
-
-    entry[...] = lax.fori_loop(0, me_ref[0], pull, init_ref[...])
+    e = init_ref[...]
+    order = order_of(got_ref.shape[0])
+    for q in range(got_ref.shape[0] - 1):
+        k = order.index(q)
+        e = jnp.where(q < me_ref[0], got_ref[k, 0:tiles, :] * e + got_ref[k, tiles : 2 * tiles, :], e)
+    entry[...] = e
     acc[...] = jnp.zeros_like(acc)
 
     def turned_state(j):
@@ -328,14 +334,13 @@
 ):
     tiles, rows, _ = fresh_ref.shape
     pairs = got_ref.shape[0]
+    order = order_of(pairs)
     moves[0] = jnp.zeros((tiles, LANE), F32)
-
-    def pull(q, d):
-        d = got_ref[q, 0:tiles, :] * d + got_ref[q, tiles : 2 * tiles, :]
+    d = moves[0]
+    for q in range(pairs - 1):
+        k = order.index(q)
+        d = got_ref[k, 0:tiles, :] * d + got_ref[k, tiles : 2 * tiles, :]
         moves[q + 1] = d
-        return d
-
-    lax.fori_loop(0, pairs - 1, pull, moves[0], unroll=True)
     entry[...] = moves[lax.div(me_ref[0], 2)]
 
     @pl.when(lax.rem(me_ref[0], 2) == 1)
@@ -350,13 +355,12 @@
         copies.append(pltpu.make_async_copy(path.at[:, here], path_hbm.at[:, here], sem.at[p]))
         copies[-1].start()
 
-    def gather(q, carry):
-        quad, sums = carry
+    quad, sums = moves[0], moves[0, 0:SUB, :]
+    for q in range(pairs):
+        k = order.index(q)
         d = moves[q]
-        quad = quad + d * (got_ref[q, 2 * tiles : 3 * tiles, :] + got_ref[q, 3 * tiles : 4 * tiles, :] * d)
-        return quad, sums + got_ref[q, 4 * tiles : 4 * tiles + SUB, :]
-
-    quad, sums = lax.fori_loop(0, pairs, gather, (moves[0], moves[0, 0:SUB, :]), unroll=True)
+        quad = quad + d * (got_ref[k, 2 * tiles : 3 * tiles, :] + got_ref[k, 3 * tiles : 4 * tiles, :] * d)
+        sums = sums + got_ref[k, 4 * tiles : 4 * tiles + SUB, :]
     extra = jnp.sum(quad, axis=0, keepdims=True)
     totals = [sums[0:1, :], sums[1:2, :], sums[2:3, :] + extra]
     for k, row in enumerate(totals):
@@ -368,8 +372,14 @@
         copy.wait()
 
 
-def exchange(pay, groups=None):
-    return lax.all_to_all(pay, "tm", 0, 0, axis_index_groups=groups)
+def order_of(count):
+    ends = [count - 1 - k // 2 if k % 2 == 0 else k // 2 for k in range(count)]
+    return ORDERS.get(count, ends)
+
+
+def exchange(pay, every):
+    order = order_of(pay.shape[0])
+    return lax.all_to_all(pay, "tm", 0, 0, axis_index_groups=[[every * k + s for k in order] for s in range(every)])
 
 
 def body(gate_in, cand_in, rates, init_state, recur_weight):
@@ -413,7 +423,7 @@
         compiler_params=pltpu.CompilerParams(vmem_limit_bytes=VMEM_LIMIT),
         name="start",
     )(me, *(pltpu.with_memory_space_constraint(x, pltpu.HBM) for x in (gate_in, cand_in, rates.reshape(1, width), init_row, recur_weight)))
-    got = exchange(pay)
+    got = exchange(pay, 1)
 
     scratch = [
         pltpu.VMEM((rows, width), F32),
@@ -430,7 +440,7 @@
         compiler_params=pltpu.CompilerParams(vmem_limit_bytes=VMEM_LIMIT),
         name="middle",
     )(me, got, init_tile, keep, base, cum_a, cum_b, diag, recur_weight)
-    got = exchange(pay)
+    got = exchange(pay, 1)
 
     fresh, cum_a, one = pl.pallas_call(
         functools.partial(step_kernel, True),
@@ -452,7 +462,7 @@
         compiler_params=pltpu.CompilerParams(vmem_limit_bytes=VMEM_LIMIT),
         name="pair",
     )(me, one, other)
-    got = exchange(pay, [[2 * k + s for k in range(peers // 2)] for s in range(2)])
+    got = exchange(pay, 2)
 
     path, norms = pl.pallas_call(
         functools.partial(final_kernel, peers * rows * width),

time: 55.4 us -> 51.5 us (0.930)
  blocking collectives: 39 us -> 35.1 us
  starting transfers between devices: 0.84 us -> 0.27 us
  waiting for transfers between devices: 3.19 us -> 3.76 us
    all_to_all x3, blocking collectives: 39 us -> 35.1 us  [exchange(): lax.all_to_all(pay, 'tm', 0, 0, axis_index_groups=[[every * k + s for k i...]
    ppermute x1, starting transfers between devices: 0.84 us -> 0.27 us  [body(): other = lax.ppermute(one, 'tm', [(k, k ^ 1) for k in range(peers)])]
    ppermute x1, waiting for transfers between devices: 3.19 us -> 3.76 us  [body(): other = lax.ppermute(one, 'tm', [(k, k ^ 1) for k in range(peers)])]
where the time goes in v5:
time: 51.5 us; the launch traced here: 51.3 us
  blocking collectives  35.1 us (68%)
  Pallas kernels  11.5 us (22%)
  waiting for transfers between devices  3.76 us (7%)
  between operations  0.68 us (1%)
    all_to_all x3, blocking collectives, exchange(): lax.all_to_all(pay, 'tm', 0, 0, axis_index_groups=[[every * k + s for k i...  35.1 us
    pallas_call x1, Pallas kernels, body(): pl.pallas_call(start_kernel, out_shape=(grid_f32, grid_f32, grid_f32, gri...  6.34 us
    ppermute x1, waiting for transfers between devices, body(): other = lax.ppermute(one, 'tm', [(k, k ^ 1) for k in range(peers)])  3.76 us
    pallas_call x1, Pallas kernels, body(): pl.pallas_call(functools.partial(step_kernel, True), out_shape=(turned, t...  2.21 us
    pallas_call x1, Pallas kernels, body(): pl.pallas_call(first_step_kernel, out_shape=(grid_f32, grid_f32, grid_f32...  2 us
  transfers between devices with their start and end apart: 1, of which 1 were waited for; matrix products, arithmetic and copies ran while one was open for 0% of the time, Pallas kernels for 0%

profile of v5, /device:TPU:0, one launch (start us, length us, event | category | flops | bytes accessed | tf_op | source)
XLA Modules:
  0.0 51.3 jit_solution(9555891646045780484)
XLA Ops:
  0.6 0.0 copy-start.1
  0.6 0.0 copy-start
  0.7 6.3 %start.1 = (f32[64,2048]{1,0:T(8,128)S(1)}, f32[64,2048]{1,0:T(8,128)S(1)}, f32[64,2048]{1,0:T(8,128)S(1)}, f32[64,2048]{1,0:T(8,128)S(1)}, f32[1,2048]{1,0:T(1,128)S(1)}, /*index=5*/f32[16,32,128]{2,1,0:T(8,128)S(1)}) custom-call(s32[1]{0:T(128)} %bitcast.me_ref.me, bf16[64,2048]{1,0:T(8,128)(2,1)} %gate_hbm.1, bf16[64,2048]{1,0:T(8,128)(2,1)} %cand_hbm.1, ...), custom_call_target="tpu_custom_call" | custom-call | tf_op jit(solution)/shard_map/start/pallas_call | solution.py:403
  7.0 13.0 %all_to_all.15.got = f32[16,32,128]{2,1,0:T(8,128)S(1)} all-to-all(f32[16,32,128]{2,1,0:T(8,128)S(1)} %get-tuple-element.16), channel_id=1, replica_groups={{22,10,26,28,20,16,12,0,6,2,8,4,14,18,30,24},{23,11,27,29,21,17,13,1,7,..., dimensions={0} | all-to-all | bytes 524288 | tf_op jit(solution)/shard_map/all_to_all | solution.py:382
  20.0 0.0 copy-done.1
  20.0 0.0 copy-done
  20.0 2.0 %middle.1 = (f32[64,2048]{1,0:T(8,128)S(1)}, f32[64,2048]{1,0:T(8,128)S(1)}, f32[64,2048]{1,0:T(8,128)S(1)}, f32[8,128]{1,0:T(8,128)S(1)}, f32[16,32,128]{2,1,0:T(8,128)S(1)}) custom-call(s32[1]{0:T(128)} %bitcast.me_ref.me, f32[16,32,128]{2,1,0:T(8,128)S(1)} %all_to_all.15.got, f32[16,128]{1,0:T(8,128)S(1)} %bitcast.5, ...), custom_call_target="tpu_custom_call" | custom-call | tf_op jit(solution)/shard_map/middle/pallas_call | solution.py:434
  22.0 11.1 %all_to_all.16.got_ref = f32[16,32,128]{2,1,0:T(8,128)S(1)} all-to-all(f32[16,32,128]{2,1,0:T(8,128)S(1)} %get-tuple-element.22), channel_id=1, replica_groups={{22,10,26,28,20,16,12,0,6,2,8,4,14,18,30,24},{23,11,27,29,21,17,13,1,7,..., dimensions={0} | all-to-all | bytes 524288 | tf_op jit(solution)/shard_map/all_to_all | solution.py:382
  33.1 2.2 %last.1 = (f32[16,64,128]{2,1,0:T(8,128)S(1)}, f32[16,64,128]{2,1,0:T(8,128)S(1)}, f32[72,128]{1,0:T(8,128)S(1)}) custom-call(s32[1]{0:T(128)} %bitcast.me_ref.me, f32[16,32,128]{2,1,0:T(8,128)S(1)} %all_to_all.16.got_ref, f32[16,128]{1,0:T(8,128)S(1)} %bitcast.6, f32[64,2048]{1,0:T(8,128)S(1)} %get-tuple-element.17.keep.keep_ref, ...), custom_call_target="tpu_custom_call" | custom-call | tf_op jit(solution)/shard_map/last/pallas_call | solution.py:445
  35.3 0.3 collective-permute-start
  35.6 3.8 %collective-permute-done.other_ref = f32[72,128]{1,0:T(8,128)S(1)} collective-permute-done((f32[72,128]{1,0:T(8,128)S(1)}, f32[72,128]{1,0:T(8,128)S(1)}, u32[]{:S(2)}, u32[]{:S(2)}) %collective-permute-start) | collective-permute-done | bytes 36896 | tf_op jit(solution)/shard_map/ppermute | solution.py:455
  39.4 11.0 %all_to_all.17.got_ref = f32[8,72,128]{2,1,0:T(8,128)S(1)} all-to-all(f32[8,72,128]{2,1,0:T(8,128)S(1)} %pair.1), channel_id=1, replica_groups={{16,0,28,12,4,24,20,8},{18,2,30,14,6,26,22,10},{17,1,29,13,5,25,21,9},{..., dimensions={0} | all-to-all | bytes 589824 | tf_op jit(solution)/shard_map/all_to_all | solution.py:382
  50.4 0.9 %final.1 = (f32[64,2048]{1,0:T(8,128)}, f32[3]{0:T(128)}) custom-call(s32[1]{0:T(128)} %bitcast.me_ref.me, f32[8,72,128]{2,1,0:T(8,128)S(1)} %all_to_all.17.got_ref, f32[72,128]{1,0:T(8,128)S(1)} %collective-permute-done.other_ref, f32[16,64,128]{2,1,0:T(8,128)S(1)} %get-tuple-element.28.fresh_ref, f32[16,64,128]{2,1,0:T(8,128)S(1)} %get-tuple-element.29.cum_a_ref), custom_call_target="tpu_custom_call" | custom-call | tf_op jit(solution)/shard_map/final/pallas_call | solution.py:467
  (1 shorter events, 0.0 us)
Async XLA Ops:
  0.6 19.3 %copy-start.1 = (f32[2048]{0:T(1024)S(1)}, f32[2048]{0:T(1024)}, u32[]{:S(2)}) copy-start(f32[2048]{0:T(1024)} %param.8) | copy-start | bytes 24580
  0.6 19.3 %copy-start = (bf16[2048,2048]{1,0:T(8,128)(2,1)S(1)}, bf16[2048,2048]{1,0:T(8,128)(2,1)}, u32[]{:S(2)}) copy-start(bf16[2048,2048]{1,0:T(8,128)(2,1)} %w_ref.1) | copy-start | bytes 25165828
  35.3 4.0 %collective-permute-start = (f32[72,128]{1,0:T(8,128)S(1)}, f32[72,128]{1,0:T(8,128)S(1)}, u32[]{:S(2)}, u32[]{:S(2)}) collective-permute-start(f32[72,128]{1,0:T(8,128)S(1)} %get-tuple-element.27.one_ref), channel_id=1, source_target_pairs={{0,2},{2,0},{4,6},{6,4},{8,10},{10,8},{12,14},{14,12},{16,18},{18,... | collective-permute-start | bytes 110600 | tf_op jit(solution)/shard_map/ppermute | solution.py:455

commit v6 on v5

--- a/solution.py
+++ b/solution.py
@@ -13,8 +13,9 @@
 PARTS = 2
 CHUNKS = 2
 ORDERS = {
-    8: [4, 0, 7, 3, 1, 6, 5, 2],
-    16: [11, 5, 13, 14, 10, 8, 6, 0, 3, 1, 4, 2, 7, 9, 15, 12],
+    (16, 0): [5, 14, 10, 8, 13, 0, 3, 1, 4, 11, 2, 7, 6, 9, 15, 12],
+    (16, 1): [9, 5, 13, 14, 10, 8, 6, 15, 2, 1, 4, 3, 7, 11, 0, 12],
+    (8, 2): [4, 0, 7, 3, 1, 6, 5, 2],
 }
 VMEM_LIMIT = 16 * 1024 * 1024
 F32 = jnp.float32
@@ -196,7 +197,7 @@
     per = WIDE // LANE
 
     e = init_ref[...]
-    order = order_of(got_ref.shape[0])
+    order = order_of(got_ref.shape[0], int(last))
     for q in range(got_ref.shape[0] - 1):
         k = order.index(q)
         e = jnp.where(q < me_ref[0], got_ref[k, 0:tiles, :] * e + got_ref[k, tiles : 2 * tiles, :], e)
@@ -334,7 +335,7 @@
 ):
     tiles, rows, _ = fresh_ref.shape
     pairs = got_ref.shape[0]
-    order = order_of(pairs)
+    order = order_of(pairs, 2)
     moves[0] = jnp.zeros((tiles, LANE), F32)
     d = moves[0]
     for q in range(pairs - 1):
@@ -372,13 +373,13 @@
         copy.wait()
 
 
-def order_of(count):
+def order_of(count, stage):
     ends = [count - 1 - k // 2 if k % 2 == 0 else k // 2 for k in range(count)]
-    return ORDERS.get(count, ends)
-
-
-def exchange(pay, every):
-    order = order_of(pay.shape[0])
+    return ORDERS.get((count, stage), ends)
+
+
+def exchange(pay, stage, every=1):
+    order = order_of(pay.shape[0], stage)
     return lax.all_to_all(pay, "tm", 0, 0, axis_index_groups=[[every * k + s for k in order] for s in range(every)])
 
 
@@ -423,7 +424,7 @@
         compiler_params=pltpu.CompilerParams(vmem_limit_bytes=VMEM_LIMIT),
         name="start",
     )(me, *(pltpu.with_memory_space_constraint(x, pltpu.HBM) for x in (gate_in, cand_in, rates.reshape(1, width), init_row, recur_weight)))
-    got = exchange(pay, 1)
+    got = exchange(pay, 0)
 
     scratch = [
         pltpu.VMEM((rows, width), F32),
@@ -462,7 +463,7 @@
         compiler_params=pltpu.CompilerParams(vmem_limit_bytes=VMEM_LIMIT),
         name="pair",
     )(me, one, other)
-    got = exchange(pay, 2)
+    got = exchange(pay, 2, every=2)
 
     path, norms = pl.pallas_call(
         functools.partial(final_kernel, peers * rows * width),

time: 51.5 us -> 50.4 us (0.979)
  blocking collectives: 35.1 us -> 34 us
  waiting for transfers between devices: 3.76 us -> 3.04 us
  starting transfers between devices: 0.27 us -> 0.98 us
    all_to_all x3, blocking collectives: 35.1 us -> 34 us  [exchange(): lax.all_to_all(pay, 'tm', 0, 0, axis_index_groups=[[every * k + s for k i...]
    ppermute x1, starting transfers between devices: 0.27 us -> 0.98 us  [body(): other = lax.ppermute(one, 'tm', [(k, k ^ 1) for k in range(peers)])]
    ppermute x1, waiting for transfers between devices: 3.76 us -> 3.04 us  [body(): other = lax.ppermute(one, 'tm', [(k, k ^ 1) for k in range(peers)])]
where the time goes in v6:
time: 50.4 us; the launch traced here: 50.2 us
  blocking collectives  34 us (67%)
  Pallas kernels  11.5 us (23%)
  waiting for transfers between devices  3.04 us (6%)
  starting transfers between devices  0.98 us (2%)
  between operations  0.68 us (1%)
    all_to_all x3, blocking collectives, exchange(): lax.all_to_all(pay, 'tm', 0, 0, axis_index_groups=[[every * k + s for k i...  34 us
    pallas_call x1, Pallas kernels, body(): pl.pallas_call(start_kernel, out_shape=(grid_f32, grid_f32, grid_f32, gri...  6.34 us
    ppermute x1, waiting for transfers between devices, body(): other = lax.ppermute(one, 'tm', [(k, k ^ 1) for k in range(peers)])  3.04 us
    pallas_call x1, Pallas kernels, body(): pl.pallas_call(functools.partial(step_kernel, True), out_shape=(turned, t...  2.21 us
    pallas_call x1, Pallas kernels, body(): pl.pallas_call(first_step_kernel, out_shape=(grid_f32, grid_f32, grid_f32...  1.99 us
  transfers between devices with their start and end apart: 1, of which 1 were waited for; matrix products, arithmetic and copies ran while one was open for 0% of the time, Pallas kernels for 0%

profile of v6, /device:TPU:0, one launch (start us, length us, event | category | flops | bytes accessed | tf_op | source)
XLA Modules:
  0.0 50.2 jit_solution(5069052387073520707)
XLA Ops:
  0.6 0.0 copy-start.1
  0.6 0.0 copy-start
  0.7 6.3 %start.1 = (f32[64,2048]{1,0:T(8,128)S(1)}, f32[64,2048]{1,0:T(8,128)S(1)}, f32[64,2048]{1,0:T(8,128)S(1)}, f32[64,2048]{1,0:T(8,128)S(1)}, f32[1,2048]{1,0:T(1,128)S(1)}, /*index=5*/f32[16,32,128]{2,1,0:T(8,128)S(1)}) custom-call(s32[1]{0:T(128)} %bitcast.me_ref.me, bf16[64,2048]{1,0:T(8,128)(2,1)} %gate_hbm.1, bf16[64,2048]{1,0:T(8,128)(2,1)} %cand_hbm.1, ...), custom_call_target="tpu_custom_call" | custom-call | tf_op jit(solution)/shard_map/start/pallas_call | solution.py:404
  7.0 12.8 %all_to_all.15.got = f32[16,32,128]{2,1,0:T(8,128)S(1)} all-to-all(f32[16,32,128]{2,1,0:T(8,128)S(1)} %get-tuple-element.16), channel_id=1, replica_groups={{10,28,20,16,26,0,6,2,8,22,4,14,12,18,30,24},{11,29,21,17,27,1,7,3,9,23..., dimensions={0} | all-to-all | bytes 524288 | tf_op jit(solution)/shard_map/all_to_all | solution.py:383
  19.8 0.0 copy-done.1
  19.8 0.0 copy-done
  19.8 2.0 %middle.1 = (f32[64,2048]{1,0:T(8,128)S(1)}, f32[64,2048]{1,0:T(8,128)S(1)}, f32[64,2048]{1,0:T(8,128)S(1)}, f32[8,128]{1,0:T(8,128)S(1)}, f32[16,32,128]{2,1,0:T(8,128)S(1)}) custom-call(s32[1]{0:T(128)} %bitcast.me_ref.me, f32[16,32,128]{2,1,0:T(8,128)S(1)} %all_to_all.15.got, f32[16,128]{1,0:T(8,128)S(1)} %bitcast.5, ...), custom_call_target="tpu_custom_call" | custom-call | tf_op jit(solution)/shard_map/middle/pallas_call | solution.py:435
  21.8 11.0 %all_to_all.16.got_ref = f32[16,32,128]{2,1,0:T(8,128)S(1)} all-to-all(f32[16,32,128]{2,1,0:T(8,128)S(1)} %get-tuple-element.22), channel_id=1, replica_groups={{18,10,26,28,20,16,12,30,4,2,8,6,14,22,0,24},{19,11,27,29,21,17,13,31,5..., dimensions={0} | all-to-all | bytes 524288 | tf_op jit(solution)/shard_map/all_to_all | solution.py:383
  32.7 2.2 %last.1 = (f32[16,64,128]{2,1,0:T(8,128)S(1)}, f32[16,64,128]{2,1,0:T(8,128)S(1)}, f32[72,128]{1,0:T(8,128)S(1)}) custom-call(s32[1]{0:T(128)} %bitcast.me_ref.me, f32[16,32,128]{2,1,0:T(8,128)S(1)} %all_to_all.16.got_ref, f32[16,128]{1,0:T(8,128)S(1)} %bitcast.6, f32[64,2048]{1,0:T(8,128)S(1)} %get-tuple-element.17.keep.keep_ref, ...), custom_call_target="tpu_custom_call" | custom-call | tf_op jit(solution)/shard_map/last/pallas_call | solution.py:446
  34.9 1.0 %collective-permute-start = (f32[72,128]{1,0:T(8,128)S(1)}, f32[72,128]{1,0:T(8,128)S(1)}, u32[]{:S(2)}, u32[]{:S(2)}) collective-permute-start(f32[72,128]{1,0:T(8,128)S(1)} %get-tuple-element.27.one_ref), channel_id=1, source_target_pairs={{0,2},{2,0},{4,6},{6,4},{8,10},{10,8},{12,14},{14,12},{16,18},{18,... | collective-permute-start | bytes 110600 | tf_op jit(solution)/shard_map/ppermute | solution.py:456
  35.9 3.0 %collective-permute-done.other_ref = f32[72,128]{1,0:T(8,128)S(1)} collective-permute-done((f32[72,128]{1,0:T(8,128)S(1)}, f32[72,128]{1,0:T(8,128)S(1)}, u32[]{:S(2)}, u32[]{:S(2)}) %collective-permute-start) | collective-permute-done | bytes 36896 | tf_op jit(solution)/shard_map/ppermute | solution.py:456
  39.0 10.2 %all_to_all.17.got_ref = f32[8,72,128]{2,1,0:T(8,128)S(1)} all-to-all(f32[8,72,128]{2,1,0:T(8,128)S(1)} %pair.1), channel_id=1, replica_groups={{16,0,28,12,4,24,20,8},{18,2,30,14,6,26,22,10},{17,1,29,13,5,25,21,9},{..., dimensions={0} | all-to-all | bytes 589824 | tf_op jit(solution)/shard_map/all_to_all | solution.py:383
  49.3 0.9 %final.1 = (f32[64,2048]{1,0:T(8,128)}, f32[3]{0:T(128)}) custom-call(s32[1]{0:T(128)} %bitcast.me_ref.me, f32[8,72,128]{2,1,0:T(8,128)S(1)} %all_to_all.17.got_ref, f32[72,128]{1,0:T(8,128)S(1)} %collective-permute-done.other_ref, f32[16,64,128]{2,1,0:T(8,128)S(1)} %get-tuple-element.28.fresh_ref, f32[16,64,128]{2,1,0:T(8,128)S(1)} %get-tuple-element.29.cum_a_ref), custom_call_target="tpu_custom_call" | custom-call | tf_op jit(solution)/shard_map/final/pallas_call | solution.py:468
  (1 shorter events, 0.0 us)
Async XLA Ops:
  0.6 19.1 %copy-start.1 = (f32[2048]{0:T(1024)S(1)}, f32[2048]{0:T(1024)}, u32[]{:S(2)}) copy-start(f32[2048]{0:T(1024)} %param.8) | copy-start | bytes 24580
  0.6 19.1 %copy-start = (bf16[2048,2048]{1,0:T(8,128)(2,1)S(1)}, bf16[2048,2048]{1,0:T(8,128)(2,1)}, u32[]{:S(2)}) copy-start(bf16[2048,2048]{1,0:T(8,128)(2,1)} %w_ref.1) | copy-start | bytes 25165828
  34.9 4.0 %collective-permute-start = (f32[72,128]{1,0:T(8,128)S(1)}, f32[72,128]{1,0:T(8,128)S(1)}, u32[]{:S(2)}, u32[]{:S(2)}) collective-permute-start(f32[72,128]{1,0:T(8,128)S(1)} %get-tuple-element.27.one_ref), channel_id=1, source_target_pairs={{0,2},{2,0},{4,6},{6,4},{8,10},{10,8},{12,14},{14,12},{16,18},{18,... | collective-permute-start | bytes 110600 | tf_op jit(solution)/shard_map/ppermute | solution.py:456

commit v7 on v6

--- a/solution.py
+++ b/solution.py
@@ -13,7 +13,7 @@
 PARTS = 2
 CHUNKS = 2
 ORDERS = {
-    (16, 0): [5, 14, 10, 8, 13, 0, 3, 1, 4, 11, 2, 7, 6, 9, 15, 12],
+    (16, 0): [5, 7, 10, 8, 13, 0, 1, 4, 11, 2, 9, 6, 3, 14, 15, 12],
     (16, 1): [9, 5, 13, 14, 10, 8, 6, 15, 2, 1, 4, 3, 7, 11, 0, 12],
     (8, 2): [4, 0, 7, 3, 1, 6, 5, 2],
 }
@@ -117,8 +117,6 @@
     mixed[...] = jnp.zeros_like(mixed)
     rates_copy.wait()
     init_copy.wait()
-    for copy in diag_copies:
-        copy.wait()
 
     @pl.when(me == 0)
     def _():
@@ -137,6 +135,8 @@
     for p in range(PARTS):
         gate_copies[p].wait()
         cand_copies[p].wait()
+        for copy in diag_copies[p * tiles // PARTS : (p + 1) * tiles // PARTS]:
+            copy.wait()
 
         @pl.loop(p * (part // WIDE), (p + 1) * (part // WIDE), unroll=True)
         def _(j):

time: 50.4 us -> 50.4 us (level)
  no operation moved by 1% of the time
where the time goes in v7:
time: 50.4 us; the launch traced here: 50.1 us
  blocking collectives  33.9 us (67%)
  Pallas kernels  11.5 us (23%)
  waiting for transfers between devices  3.04 us (6%)
  starting transfers between devices  0.98 us (2%)
  between operations  0.68 us (1%)
    all_to_all x3, blocking collectives, exchange(): lax.all_to_all(pay, 'tm', 0, 0, axis_index_groups=[[every * k + s for k i...  33.9 us
    pallas_call x1, Pallas kernels, body(): pl.pallas_call(start_kernel, out_shape=(grid_f32, grid_f32, grid_f32, gri...  6.36 us
    ppermute x1, waiting for transfers between devices, body(): other = lax.ppermute(one, 'tm', [(k, k ^ 1) for k in range(peers)])  3.04 us
    pallas_call x1, Pallas kernels, body(): pl.pallas_call(functools.partial(step_kernel, True), out_shape=(turned, t...  2.21 us
    pallas_call x1, Pallas kernels, body(): pl.pallas_call(first_step_kernel, out_shape=(grid_f32, grid_f32, grid_f32...  2 us
  transfers between devices with their start and end apart: 1, of which 1 were waited for; matrix products, arithmetic and copies ran while one was open for 0% of the time, Pallas kernels for 0%

profile of v7, /device:TPU:0, one launch (start us, length us, event | category | flops | bytes accessed | tf_op | source)
XLA Modules:
  0.0 50.1 jit_solution(11503074137268756801)
XLA Ops:
  0.6 0.0 copy-start.1
  0.6 0.0 copy-start
  0.7 6.4 %start.1 = (f32[64,2048]{1,0:T(8,128)S(1)}, f32[64,2048]{1,0:T(8,128)S(1)}, f32[64,2048]{1,0:T(8,128)S(1)}, f32[64,2048]{1,0:T(8,128)S(1)}, f32[1,2048]{1,0:T(1,128)S(1)}, /*index=5*/f32[16,32,128]{2,1,0:T(8,128)S(1)}) custom-call(s32[1]{0:T(128)} %bitcast.me_ref.me, bf16[64,2048]{1,0:T(8,128)(2,1)} %gate_hbm.1, bf16[64,2048]{1,0:T(8,128)(2,1)} %cand_hbm.1, ...), custom_call_target="tpu_custom_call" | custom-call | tf_op jit(solution)/shard_map/start/pallas_call | solution.py:404
  7.0 12.9 %all_to_all.15.got = f32[16,32,128]{2,1,0:T(8,128)S(1)} all-to-all(f32[16,32,128]{2,1,0:T(8,128)S(1)} %get-tuple-element.16), channel_id=1, replica_groups={{10,14,20,16,26,0,2,8,22,4,18,12,6,28,30,24},{11,15,21,17,27,1,3,9,23,5..., dimensions={0} | all-to-all | bytes 524288 | tf_op jit(solution)/shard_map/all_to_all | solution.py:383
  19.9 0.0 copy-done.1
  19.9 0.0 copy-done
  19.9 2.0 %middle.1 = (f32[64,2048]{1,0:T(8,128)S(1)}, f32[64,2048]{1,0:T(8,128)S(1)}, f32[64,2048]{1,0:T(8,128)S(1)}, f32[8,128]{1,0:T(8,128)S(1)}, f32[16,32,128]{2,1,0:T(8,128)S(1)}) custom-call(s32[1]{0:T(128)} %bitcast.me_ref.me, f32[16,32,128]{2,1,0:T(8,128)S(1)} %all_to_all.15.got, f32[16,128]{1,0:T(8,128)S(1)} %bitcast.5, ...), custom_call_target="tpu_custom_call" | custom-call | tf_op jit(solution)/shard_map/middle/pallas_call | solution.py:435
  21.9 10.8 %all_to_all.16.got_ref = f32[16,32,128]{2,1,0:T(8,128)S(1)} all-to-all(f32[16,32,128]{2,1,0:T(8,128)S(1)} %get-tuple-element.22), channel_id=1, replica_groups={{18,10,26,28,20,16,12,30,4,2,8,6,14,22,0,24},{19,11,27,29,21,17,13,31,5..., dimensions={0} | all-to-all | bytes 524288 | tf_op jit(solution)/shard_map/all_to_all | solution.py:383
  32.7 2.2 %last.1 = (f32[16,64,128]{2,1,0:T(8,128)S(1)}, f32[16,64,128]{2,1,0:T(8,128)S(1)}, f32[72,128]{1,0:T(8,128)S(1)}) custom-call(s32[1]{0:T(128)} %bitcast.me_ref.me, f32[16,32,128]{2,1,0:T(8,128)S(1)} %all_to_all.16.got_ref, f32[16,128]{1,0:T(8,128)S(1)} %bitcast.6, f32[64,2048]{1,0:T(8,128)S(1)} %get-tuple-element.17.keep.keep_ref, ...), custom_call_target="tpu_custom_call" | custom-call | tf_op jit(solution)/shard_map/last/pallas_call | solution.py:446
  34.9 1.0 %collective-permute-start = (f32[72,128]{1,0:T(8,128)S(1)}, f32[72,128]{1,0:T(8,128)S(1)}, u32[]{:S(2)}, u32[]{:S(2)}) collective-permute-start(f32[72,128]{1,0:T(8,128)S(1)} %get-tuple-element.27.one_ref), channel_id=1, source_target_pairs={{0,2},{2,0},{4,6},{6,4},{8,10},{10,8},{12,14},{14,12},{16,18},{18,... | collective-permute-start | bytes 110600 | tf_op jit(solution)/shard_map/ppermute | solution.py:456
  35.9 3.0 %collective-permute-done.other_ref = f32[72,128]{1,0:T(8,128)S(1)} collective-permute-done((f32[72,128]{1,0:T(8,128)S(1)}, f32[72,128]{1,0:T(8,128)S(1)}, u32[]{:S(2)}, u32[]{:S(2)}) %collective-permute-start) | collective-permute-done | bytes 36896 | tf_op jit(solution)/shard_map/ppermute | solution.py:456
  39.0 10.2 %all_to_all.17.got_ref = f32[8,72,128]{2,1,0:T(8,128)S(1)} all-to-all(f32[8,72,128]{2,1,0:T(8,128)S(1)} %pair.1), channel_id=1, replica_groups={{16,0,28,12,4,24,20,8},{18,2,30,14,6,26,22,10},{17,1,29,13,5,25,21,9},{..., dimensions={0} | all-to-all | bytes 589824 | tf_op jit(solution)/shard_map/all_to_all | solution.py:383
  49.2 0.9 %final.1 = (f32[64,2048]{1,0:T(8,128)}, f32[3]{0:T(128)}) custom-call(s32[1]{0:T(128)} %bitcast.me_ref.me, f32[8,72,128]{2,1,0:T(8,128)S(1)} %all_to_all.17.got_ref, f32[72,128]{1,0:T(8,128)S(1)} %collective-permute-done.other_ref, f32[16,64,128]{2,1,0:T(8,128)S(1)} %get-tuple-element.28.fresh_ref, f32[16,64,128]{2,1,0:T(8,128)S(1)} %get-tuple-element.29.cum_a_ref), custom_call_target="tpu_custom_call" | custom-call | tf_op jit(solution)/shard_map/final/pallas_call | solution.py:468
  (1 shorter events, 0.0 us)
Async XLA Ops:
  0.6 19.3 %copy-start.1 = (f32[2048]{0:T(1024)S(1)}, f32[2048]{0:T(1024)}, u32[]{:S(2)}) copy-start(f32[2048]{0:T(1024)} %param.8) | copy-start | bytes 24580
  0.6 19.3 %copy-start = (bf16[2048,2048]{1,0:T(8,128)(2,1)S(1)}, bf16[2048,2048]{1,0:T(8,128)(2,1)}, u32[]{:S(2)}) copy-start(bf16[2048,2048]{1,0:T(8,128)(2,1)} %w_ref.1) | copy-start | bytes 25165828
  34.9 4.0 %collective-permute-start = (f32[72,128]{1,0:T(8,128)S(1)}, f32[72,128]{1,0:T(8,128)S(1)}, u32[]{:S(2)}, u32[]{:S(2)}) collective-permute-start(f32[72,128]{1,0:T(8,128)S(1)} %get-tuple-element.27.one_ref), channel_id=1, source_target_pairs={{0,2},{2,0},{4,6},{6,4},{8,10},{10,8},{12,14},{14,12},{16,18},{18,... | collective-permute-start | bytes 110600 | tf_op jit(solution)/shard_map/ppermute | solution.py:456
